TPU v7x, 32 devices: a whole 2x2x4 slice. The times are simulated.
32 devices in a mesh: emb: 4 (over z), col: 2 (over y), row: 4 (over x, core).
Axes of the slice: x: 2, y: 2, z: 4, core: 2. Of those that a mesh axis runs over, the one named last changes fastest.
Arguments:
- inter_mask: int32 [1024, 32768], P('row', 'col')
- emb_user: bfloat16 [1024, 64], P(('row', 'col'), 'emb')
- emb_item: bfloat16 [32768, 64], P(('col', 'row'), 'emb')
- triples: int32 [4096, 3], replicated
Outputs:
- output 1: bfloat16 [1024, 64], P(('row', 'col'), 'emb')
- output 2: bfloat16 [32768, 64], P(('col', 'row'), 'emb')
- output 3: float32 [4096], replicated
All inputs are finite; a program needn't handle non-finite values.
Results may differ from a plain program's by a relative error of at most 0.0133188.
Values are sent between devices in bfloat16 or wider.
A program may use at most 1 GiB of HBM per device.

v0:
```python
import jax
import jax.numpy as jnp
from jax import lax
from jax.sharding import PartitionSpec as P

NUM_LAYERS = 3


def lookup_rows(table, ids, offset):
    own_rows = table.shape[0]
    local_ids = ids - offset
    owned = (local_ids >= 0) & (local_ids < own_rows)
    picked = jnp.take(table, jnp.clip(local_ids, 0, own_rows - 1), axis=0)
    return jnp.where(owned[:, None], picked.astype(jnp.float32), 0.0)


def bpr_terms(final_user, final_item, triples, user_off, item_off):
    num_trip = triples.shape[0]
    fetched = jnp.concatenate([
        lookup_rows(final_user, triples[:, 0], user_off),
        lookup_rows(final_item, triples[:, 1], item_off),
        lookup_rows(final_item, triples[:, 2], item_off)], axis=0)
    fetched = lax.psum(fetched, ("row", "col"))
    e_user = fetched[:num_trip]
    e_pos = fetched[num_trip:2 * num_trip]
    e_neg = fetched[2 * num_trip:]
    score = lax.psum(jnp.sum(e_user * (e_pos - e_neg), axis=1), "emb")
    return jax.nn.softplus(-score)


def norm_adjacency(mask_blk):
    deg_user = lax.psum(jnp.sum(mask_blk, axis=1), "col")
    deg_item = lax.psum(jnp.sum(mask_blk, axis=0), "row")
    inv_user = lax.rsqrt(jnp.maximum(deg_user, 1).astype(jnp.float32))
    inv_item = lax.rsqrt(jnp.maximum(deg_item, 1).astype(jnp.float32))
    return ((inv_user[:, None] * mask_blk.astype(jnp.float32)) * inv_item[None, :]).astype(jnp.bfloat16)


def solution(mesh):
    n_col = mesh.shape["col"]
    n_row = mesh.shape["row"]

    def local_fn(mask_blk, user_sh, item_sh, triples):
        adj_blk = norm_adjacency(mask_blk)
        user_cur = user_sh
        item_cur = item_sh
        user_acc = user_sh.astype(jnp.float32)
        item_acc = item_sh.astype(jnp.float32)
        for layer_idx in range(NUM_LAYERS):
            item_panel = lax.all_gather(item_cur, "row", axis=0, tiled=True)
            user_part = jnp.dot(adj_blk, item_panel, preferred_element_type=jnp.float32)
            user_next = lax.psum_scatter(user_part, "col", scatter_dimension=0, tiled=True).astype(jnp.bfloat16)
            user_panel = lax.all_gather(user_cur, "col", axis=0, tiled=True)
            item_part = lax.dot_general(adj_blk, user_panel, (((0,), (0,)), ((), ())), preferred_element_type=jnp.float32)
            item_next = lax.psum_scatter(item_part, "row", scatter_dimension=0, tiled=True).astype(jnp.bfloat16)
            user_acc = user_acc + user_next.astype(jnp.float32)
            item_acc = item_acc + item_next.astype(jnp.float32)
            user_cur = user_next
            item_cur = item_next
        final_user = (user_acc / (NUM_LAYERS + 1)).astype(jnp.bfloat16)
        final_item = (item_acc / (NUM_LAYERS + 1)).astype(jnp.bfloat16)
        user_off = (lax.axis_index("row") * n_col + lax.axis_index("col")) * final_user.shape[0]
        item_off = (lax.axis_index("col") * n_row + lax.axis_index("row")) * final_item.shape[0]
        return final_user, final_item, bpr_terms(final_user, final_item, triples, user_off, item_off)

    return jax.shard_map(
        local_fn, mesh=mesh,
        in_specs=(P("row", "col"), P(("row", "col"), "emb"), P(("col", "row"), "emb"), P()),
        out_specs=(P(("row", "col"), "emb"), P(("col", "row"), "emb"), P()),
        check_vma=False)
```

profile of v0, /device:TPU:0, one launch (start us, length us, event | category | flops | bytes accessed | tf_op | source)
XLA Modules:
  0.0 333.0 jit_solution(9128832063361054554)
XLA Ops:
  7.2 9.2 %fusion.4 = (s32[256]{0:T(256)S(1)}, s32[16384]{0:T(1024)}) fusion(s32[256,16384]{1,0:T(8,128)} %param.6), kind=kLoop, calls=%fused_computation.33 | loop fusion | flops 8371968 | bytes 16843776 | tf_op jit(solution)/shard_map/reduce_sum | solution.py:32
  16.5 0.0 reduce-scatter.7.cloned.1.call-start
  16.5 5.3 %psum.28 = s32[256]{0:T(256)S(1)} all-reduce(s32[256]{0:T(256)S(1)} %get-tuple-element.4), channel_id=1, replica_groups=mesh['emb'=4,'col'=2,'row'=4] {'col'}, use_global_device_ids=true, to_apply=%region_1.0 | all-reduce | flops 256 | bytes 2048 | tf_op jit(solution)/shard_map/psum | solution.py:32
  21.9 7.9 %all_gather.18 = bf16[16384,16]{0,1:T(8,128)(2,1)S(1)} all-gather(bf16[4096,16]{0,1:T(8,128)(2,1)S(1)} %copy-done.2), channel_id=1, replica_groups=mesh['emb'=4,'col'=2,'row'=4] {'row'}, dimensions={0}, use_global_device_ids=true | all-gather | bytes 655360 | tf_op jit(solution)/shard_map/all_gather | solution.py:50
  29.8 4.3 %all_gather.19 = bf16[256,16]{0,1:T(8,128)(2,1)S(1)} all-gather(bf16[128,16]{0,1:T(8,128)(2,1)S(1)} %copy-done.9), channel_id=1, replica_groups=mesh['emb'=4,'col'=2,'row'=4] {'col'}, dimensions={0}, use_global_device_ids=true | all-gather | bytes 12288 | tf_op jit(solution)/shard_map/all_gather | solution.py:53
  34.1 16.8 %all-reduce.3.cloned.1.call-done = s32[16384]{0:T(1024)} async-done(((s32[16384]{0:T(1024)}), s32[16384]{0:T(1024)}) %all-reduce.3.cloned.1.call-update) | async-done | bytes 65552 | tf_op jit(solution)/shard_map/psum | solution.py:33
  50.9 0.9 convert_rsqrt_fusion
  51.7 7.1 %multiply_convert_fusion = bf16[256,16384]{1,0:T(8,128)(2,1)S(1)} fusion(s32[256,16384]{1,0:T(8,128)} %param.6, f32[16384]{0:T(1024)S(1)} %convert_rsqrt_fusion, f32[256]{0:T(256)S(1)} %convert_rsqrt_fusion.1), kind=kLoop, calls=%fused_computation.3 | loop fusion | flops 16777216 | bytes 25232384 | tf_op jit(solution)/shard_map/convert_element_type | solution.py:36
  58.9 3.2 copy-done
  62.1 2.9 fusion.5
  65.0 0.0 reduce-scatter.9.cloned.1.call-start
  65.0 5.7 %fusion.8 = f32[16384,16]{0,1:T(8,128)} fusion(bf16[256,16]{0,1:T(8,128)(2,1)S(1)} %all_gather.19, bf16[256,16384]{1,0:T(8,128)(2,1)} %copy-done), kind=kOutput, calls=%fused_computation.37 | convolution fusion | flops 134217728 | bytes 9445376 | tf_op jit(solution)/shard_map/dot_general | solution.py:54
  70.8 4.3 %reduce-scatter.7.cloned.1.call-done = f32[128,16]{0,1:T(8,128)} async-done(((f32[256,16]{0,1:T(8,128)}), f32[128,16]{0,1:T(8,128)}) %reduce-scatter.7.cloned.1.call-update) | async-done | bytes 8208 | tf_op jit(solution)/shard_map/reduce_scatter | solution.py:52
  75.1 0.7 convert_element_type.74
  75.8 4.3 %all_gather.21 = bf16[256,16]{0,1:T(8,128)(2,1)S(1)} all-gather(bf16[128,16]{0,1:T(8,128)(2,1)S(1)} %convert_element_type.74), channel_id=1, replica_groups=mesh['emb'=4,'col'=2,'row'=4] {'col'}, dimensions={0}, use_global_device_ids=true | all-gather | bytes 12288 | tf_op jit(solution)/shard_map/all_gather | solution.py:53
  80.1 22.2 %reduce-scatter.9.cloned.1.call-done = f32[4096,16]{0,1:T(8,128)} async-done(((f32[16384,16]{0,1:T(8,128)}), f32[4096,16]{0,1:T(8,128)}) %reduce-scatter.9.cloned.1.call-update) | async-done | bytes 262160 | tf_op jit(solution)/shard_map/reduce_scatter | solution.py:55
  102.3 1.0 convert_element_type.76
  103.3 6.5 %all_gather.20 = bf16[16384,16]{0,1:T(8,128)(2,1)S(1)} all-gather(bf16[4096,16]{0,1:T(8,128)(2,1)S(1)} %convert_element_type.76), channel_id=1, replica_groups=mesh['emb'=4,'col'=2,'row'=4] {'row'}, dimensions={0}, use_global_device_ids=true | all-gather | bytes 655360 | tf_op jit(solution)/shard_map/all_gather | solution.py:50
  109.8 6.3 %fusion.6 = f32[256,16]{0,1:T(8,128)} fusion(bf16[256,16384]{1,0:T(8,128)(2,1)} %copy-done, bf16[16384,16]{0,1:T(8,128)(2,1)S(1)} %all_gather.20), kind=kOutput, calls=%fused_computation.35 | convolution fusion | flops 134217728 | bytes 8929280 | tf_op jit(solution)/shard_map/dot_general | solution.py:51
  116.2 5.7 %fusion.9 = f32[16384,16]{0,1:T(8,128)} fusion(bf16[256,16]{0,1:T(8,128)(2,1)S(1)} %all_gather.21, bf16[256,16384]{1,0:T(8,128)(2,1)} %copy-done), kind=kOutput, calls=%fused_computation.38 | convolution fusion | flops 134217728 | bytes 9445376 | tf_op jit(solution)/shard_map/dot_general | solution.py:54
  122.0 4.9 %reduce-scatter.11.cloned.1.call-done = f32[128,16]{0,1:T(8,128)} async-done(((f32[256,16]{0,1:T(8,128)}), f32[128,16]{0,1:T(8,128)}) %reduce-scatter.11.cloned.1.call-update) | async-done | bytes 8208 | tf_op jit(solution)/shard_map/reduce_scatter | solution.py:52
  126.8 0.7 convert_element_type.77
  127.5 4.5 %all_gather.23 = bf16[256,16]{0,1:T(8,128)(2,1)S(1)} all-gather(bf16[128,16]{0,1:T(8,128)(2,1)S(1)} %convert_element_type.77), channel_id=1, replica_groups=mesh['emb'=4,'col'=2,'row'=4] {'col'}, dimensions={0}, use_global_device_ids=true | all-gather | bytes 12288 | tf_op jit(solution)/shard_map/all_gather | solution.py:53
  132.0 5.6 %fusion.10 = f32[16384,16]{0,1:T(8,128)} fusion(bf16[256,16]{0,1:T(8,128)(2,1)S(1)} %all_gather.23, bf16[256,16384]{1,0:T(8,128)(2,1)} %copy-done), kind=kOutput, calls=%fused_computation.39 | convolution fusion | flops 134217728 | bytes 9445376 | tf_op jit(solution)/shard_map/dot_general | solution.py:54
  137.6 0.0 reduce-scatter.15.cloned.1.call-start
  137.7 0.1 broadcast_clamp_fusion.2
  137.8 0.9 and_reduce_fusion.2
  138.7 15.2 %reduce-scatter.13.cloned.1.call-done = f32[4096,16]{0,1:T(8,128)} async-done(((f32[16384,16]{0,1:T(8,128)}), f32[4096,16]{0,1:T(8,128)}) %reduce-scatter.13.cloned.1.call-update) | async-done | bytes 262160 | tf_op jit(solution)/shard_map/reduce_scatter | solution.py:55
  153.9 27.1 %reduce-scatter.17.cloned.1.call-done = f32[4096,16]{0,1:T(8,128)} async-done(((f32[16384,16]{0,1:T(8,128)}), f32[4096,16]{0,1:T(8,128)}) %reduce-scatter.17.cloned.1.call-update) | async-done | bytes 262160 | tf_op jit(solution)/shard_map/reduce_scatter | solution.py:55
  181.0 1.1 multiply_convert_fusion.1
  182.1 6.5 %all_gather.22 = bf16[16384,16]{0,1:T(8,128)(2,1)S(1)} all-gather(bf16[4096,16]{0,1:T(8,128)(2,1)S(1)} %get-tuple-element.12), channel_id=1, replica_groups=mesh['emb'=4,'col'=2,'row'=4] {'row'}, dimensions={0}, use_global_device_ids=true | all-gather | bytes 655360 | tf_op jit(solution)/shard_map/all_gather | solution.py:50
  188.6 6.3 %fusion.7 = f32[256,16]{0,1:T(8,128)} fusion(bf16[256,16384]{1,0:T(8,128)(2,1)} %copy-done, bf16[16384,16]{0,1:T(8,128)(2,1)S(1)} %all_gather.22), kind=kOutput, calls=%fused_computation.36 | convolution fusion | flops 134217728 | bytes 8929280 | tf_op jit(solution)/shard_map/dot_general | solution.py:51
  194.9 0.5 copy.11
  195.4 12.1 %gather_fusion.2 = bf16[4096,16]{1,0:T(8,128)(2,1)S(1)} fusion(bf16[4096,16]{1,0:T(8,128)(2,1)S(1)} %copy.11, s32[4096]{0:T(1024)S(1)} %fusion.3), kind=kCustom, calls=%fused_computation.1.clone | custom fusion | bytes 278528 | tf_op jit(solution)/shard_map/jit(_take)/gather | solution.py:13
  207.6 14.9 %gather_fusion.1 = bf16[4096,16]{1,0:T(8,128)(2,1)} fusion(bf16[4096,16]{1,0:T(8,128)(2,1)S(1)} %copy.11, s32[4096]{0:T(1024)S(1)} %fusion.2), kind=kCustom, calls=%fused_computation.clone | custom fusion | bytes 278528 | tf_op jit(solution)/shard_map/jit(_take)/gather | solution.py:13
  222.5 7.0 %convert_select_fusion = (f32[4096,16]{1,0:T(8,128)}, f32[4096,16]{1,0:T(8,128)S(1)}) fusion(bf16[4096,16]{1,0:T(8,128)(2,1)S(1)} %gather_fusion.2, pred[4096]{0:T(1024)(128)(4,1)S(1)} %compare_and_fusion, pred[4096]{0:T(1024)(128)(4,1)S(1)} %get-tuple-element.14, bf16[4096,16]{1,0:T(8,128)(2,1)} %gather_fusion.1, pred[4096]{0:T(1024)(128)(4,1)S(1)} %compare_and_fusion.1, ...), kind=kLoop, calls=%fused_computation.4 | loop fusion | flops 393216 | bytes 802816 | tf_op jit(solution)/shard_map/jit(_where)/select_n | solution.py:14
  229.5 2.2 copy.15
  231.7 1.3 copy.14
  233.0 0.7 multiply_convert_fusion.2
  233.7 0.1 copy.10
  233.8 12.1 %gather_fusion = bf16[4096,16]{1,0:T(8,128)(2,1)S(1)} fusion(bf16[128,16]{1,0:T(8,128)(2,1)S(1)} %copy.10, s32[4096]{0:T(1024)S(1)} %broadcast_clamp_fusion), kind=kCustom, calls=%fused_computation.2 | custom fusion | bytes 278528 | tf_op jit(solution)/shard_map/jit(_take)/gather | solution.py:13
  246.0 1.3 convert_select_fusion.2
  247.2 0.6 copy.13
  247.8 1.9 pad_maximum_fusion
  249.7 55.9 %all-reduce.5.cloned.1.call-done = f32[12288,16]{0,1:T(8,128)} async-done(((f32[12288,16]{0,1:T(8,128)}), f32[12288,16]{0,1:T(8,128)}) %all-reduce.5.cloned.1.call-update) | async-done | bytes 786448 | tf_op jit(solution)/shard_map/psum | solution.py:23
  305.7 1.2 fusion.1
  306.8 18.7 %psum.31 = f32[4096]{0:T(1024)S(1)} all-reduce(f32[4096]{0:T(1024)S(1)} %fusion.1), channel_id=1, replica_groups=mesh['emb'=4,'col'=2,'row'=4] {'emb'}, use_global_device_ids=true, to_apply=%region_12.14 | all-reduce | flops 4096 | bytes 32768 | tf_op jit(solution)/shard_map/psum | solution.py:27
  325.6 0.6 compare_select_fusion.3
  (43 shorter events, 0.4 us)
Async XLA Ops:
  7.2 14.7 %copy-start.2 = (bf16[4096,16]{0,1:T(8,128)(2,1)S(1)}, bf16[4096,16]{0,1:T(8,128)(2,1)}, u32[]{:S(2)}) copy-start(bf16[4096,16]{0,1:T(8,128)(2,1)} %param.8) | copy-start | bytes 393220
  7.2 22.6 %copy-start.9 = (bf16[128,16]{0,1:T(8,128)(2,1)S(1)}, bf16[128,16]{0,1:T(8,128)(2,1)}, u32[]{:S(2)}) copy-start(bf16[128,16]{0,1:T(8,128)(2,1)} %param.7) | copy-start | bytes 12292
  7.2 43.7 %all-reduce.3.cloned.1.call-start = ((), (), s32[]{:S(2)}) async-start(), calls=%async_computation.6 | async-start | bytes 131072 | tf_op jit(solution)/shard_map/psum | solution.py:33
  16.5 58.6 %reduce-scatter.7.cloned.1.call-start = ((), (), s32[]{:S(2)}) async-start(), calls=%async_computation.7 | async-start | bytes 24576 | tf_op jit(solution)/shard_map/reduce_scatter | solution.py:52
  58.9 3.2 copy-start
  65.0 37.3 %reduce-scatter.9.cloned.1.call-start = ((), (), s32[]{:S(2)}) async-start(), calls=%async_computation.8 | async-start | bytes 1310720 | tf_op jit(solution)/shard_map/reduce_scatter | solution.py:55
  70.7 56.1 %reduce-scatter.11.cloned.1.call-start = ((), (), s32[]{:S(2)}) async-start(), calls=%async_computation.9 | async-start | bytes 24576 | tf_op jit(solution)/shard_map/reduce_scatter | solution.py:52
  116.1 21.6 %copy-start.4 = (s32[4096,3]{0,1:T(4,128)S(1)}, s32[4096,3]{0,1:T(4,128)}, u32[]{:S(2)}) copy-start(s32[4096,3]{0,1:T(4,128)} %param.9) | copy-start | bytes 147460
  116.1 64.9 %copy-start.1 = (f32[4096,16]{0,1:T(8,128)S(1)}, f32[4096,16]{0,1:T(8,128)}, u32[]{:S(2)}) copy-start(f32[4096,16]{0,1:T(8,128)} %reduce-scatter.9.cloned.1.call-done) | copy-start | bytes 786436
  116.1 37.8 %reduce-scatter.13.cloned.1.call-start = ((), (), s32[]{:S(2)}) async-start(), calls=%async_computation.10 | async-start | bytes 1310720 | tf_op jit(solution)/shard_map/reduce_scatter | solution.py:55
  121.9 59.1 %reduce-scatter.17.cloned.1.call-start = ((), (), s32[]{:S(2)}) async-start(), calls=%async_computation.12 | async-start | bytes 1310720 | tf_op jit(solution)/shard_map/reduce_scatter | solution.py:55
  137.6 95.3 %reduce-scatter.15.cloned.1.call-start = ((), (), s32[]{:S(2)}) async-start(), calls=%async_computation.11 | async-start | bytes 24576 | tf_op jit(solution)/shard_map/reduce_scatter | solution.py:52
  182.1 25.5 %copy-start.3 = (bf16[4096,16]{0,1:T(8,128)(2,1)}, bf16[4096,16]{0,1:T(8,128)(2,1)S(1)}, u32[]{:S(2)}) copy-start(bf16[4096,16]{0,1:T(8,128)(2,1)S(1)} %get-tuple-element.11) | copy-start | bytes 393220
  194.9 110.8 %all-reduce.5.cloned.1.call-start = ((), (), s32[]{:S(2)}) async-start(), calls=%async_computation.13 | async-start | bytes 1572864 | tf_op jit(solution)/shard_map/psum | solution.py:23
  222.5 10.5 %copy-start.5 = (f32[128,16]{0,1:T(8,128)S(1)}, f32[128,16]{0,1:T(8,128)}, u32[]{:S(2)}) copy-start(f32[128,16]{0,1:T(8,128)} %reduce-scatter.7.cloned.1.call-done) | copy-start | bytes 24580
  222.5 10.5 %copy-start.6 = (f32[128,16]{0,1:T(8,128)S(1)}, f32[128,16]{0,1:T(8,128)}, u32[]{:S(2)}) copy-start(f32[128,16]{0,1:T(8,128)} %reduce-scatter.11.cloned.1.call-done) | copy-start | bytes 24580
  222.5 10.5 %copy-start.10 = (bf16[128,16]{0,1:T(8,128)(2,1)S(1)}, bf16[128,16]{0,1:T(8,128)(2,1)}, u32[]{:S(2)}) copy-start(bf16[128,16]{0,1:T(8,128)(2,1)} %param.7) | copy-start | bytes 12292
  229.5 16.5 %copy-start.7 = (pred[4096]{0:T(1024)(128)(4,1)S(1)}, pred[4096]{0:T(1024)(128)(4,1)}, u32[]{:S(2)}) copy-start(pred[4096]{0:T(1024)(128)(4,1)} %get-tuple-element.9) | copy-start | bytes 12292
  229.5 16.5 %copy-start.8 = (pred[4096]{0:T(1024)(128)(4,1)S(1)}, pred[4096]{0:T(1024)(128)(4,1)}, u32[]{:S(2)}) copy-start(pred[4096]{0:T(1024)(128)(4,1)} %get-tuple-element.15) | copy-start | bytes 12292
  233.7 16.0 %copy-start.11 = (bf16[128,16]{0,1:T(8,128)(2,1)}, bf16[128,16]{0,1:T(8,128)(2,1)S(1)}, u32[]{:S(2)}) copy-start(bf16[128,16]{0,1:T(8,128)(2,1)S(1)} %multiply_convert_fusion.2) | copy-start | bytes 12292
Sparse Core Ops, SparseCore 0:
  16.6 34.2 all-reduce.2
  65.1 9.9 reduce-scatter.6
  77.6 24.6 reduce-scatter.8
  116.2 10.5 reduce-scatter.10
  129.2 24.6 reduce-scatter.12
  156.3 24.6 reduce-scatter.16
  195.0 10.5 reduce-scatter.14
  249.8 55.7 all-reduce.4
where the time goes:
time: 334 us; the launch traced here: 333 us
  waiting for transfers between devices  147 us (44%)
  blocking collectives  58.1 us (17%)
  local copies, waits for them, and re-layouts  47.1 us (14%)
  other arithmetic  34.3 us (10%)
  matrix products  32.3 us (10%)
  between operations  14.3 us (4%)
    reduce_scatter x3, waiting for transfers between devices, local_fn(): lax.psum_scatter(item_part, 'row', scatter_dimension=0, tiled=True)  64.5 us
    psum x1, waiting for transfers between devices, bpr_terms(): fetched = lax.psum(fetched, ('row', 'col'))  55.9 us
    gather x3, local copies, waits for them, and re-layouts, lookup_rows(): picked = jnp.take(table, jnp.clip(local_ids, 0, own_rows - 1), axis=0)  39.2 us
    all_gather x3, blocking collectives, local_fn(): item_panel = lax.all_gather(item_cur, 'row', axis=0, tiled=True)  20.9 us
    psum x1, blocking collectives, bpr_terms(): score = lax.psum(jnp.sum(e_user * (e_pos - e_neg), axis=1), 'emb')  18.7 us
    dot_general x3, matrix products, local_fn(): lax.dot_general(adj_blk, user_panel, (((0,), (0,)), ((), ())), preferred_...  16.9 us
    psum x1, waiting for transfers between devices, norm_adjacency(): deg_item = lax.psum(jnp.sum(mask_blk, axis=0), 'row')  16.8 us
    dot_general x3, matrix products, local_fn(): user_part = jnp.dot(adj_blk, item_panel, preferred_element_type=jnp.float32)  15.4 us
  transfers between devices with their start and end apart: 8, of which 7 were waited for; matrix products, arithmetic and copies ran while one was open for 17% of the time, Pallas kernels for 0%

commit v1 on v0

v1 whole, which is shorter than its diff:
```python
import functools

import jax
import jax.numpy as jnp
from jax import lax
from jax.experimental import pallas as pl
from jax.experimental.pallas import tpu as pltpu
from jax.sharding import PartitionSpec as P

NUM_LAYERS = 3
MESH = pl.DeviceIdType.MESH
F32 = jnp.float32
BF16 = jnp.bfloat16

NQ = 4
NS = 4
LB = 256
GL = 256


class Copies:
    def __init__(self, send_sems, recv_sems):
        self.send_sems, self.recv_sems, self.started = send_sems, recv_sems, []

    def send(self, src, dst, device):
        k = len(self.started)
        copy = pltpu.make_async_remote_copy(
            src_ref=src, dst_ref=dst, send_sem=self.send_sems.at[k],
            recv_sem=self.recv_sems.at[k], device_id=device, device_id_type=MESH)
        copy.start()
        self.started.append(copy)
        return copy

    def drain(self):
        for copy in self.started:
            copy.wait_send()


NUM_SEMS = 120


def kernel(mask_hbm, u0_ref, i0_ref, trip_ref, outu_ref, outi_ref, loss_ref,
           maskv, adj, csum, crd, crx, cch, invi, racc, rsum, rrecv, invu,
           upan, upart, urecv, ipan, ipart, ird, irx, isum,
           ohp, ohn, ohu, hip, hin, hiu, gpart, gsum, grd, grx, gry, eu, zbuf, lossb,
           mask_sems, send_sems, recv_sems):
    users = maskv.shape[1]
    quarter = maskv.shape[2]
    own_users = u0_ref.shape[1]
    sc = quarter // NS
    home = ohp.shape[2]

    z = lax.axis_index("emb")
    y = lax.axis_index("col")
    r = lax.axis_index("row")
    x = r // 2
    c = r % 2
    nz = 4

    def rel(m):
        xx = x if m < 2 else 1 - x
        cc = c if m % 2 == 0 else 1 - c
        return 2 * xx + cc

    dev_d = (z, y, rel(1))
    dev_x = (z, y, rel(2))
    dev_xd = (z, y, rel(3))
    dev_y = (z, 1 - y, r)
    dev_z = [((z + k) % nz, y, r) for k in (1, 2, 3)]

    cp = Copies(send_sems, recv_sems)

    mask_copies = {}
    for m in (3, 2, 1, 0):
        off = pl.multiple_of(rel(m) * quarter, quarter)
        mc = pltpu.make_async_copy(mask_hbm.at[:, pl.ds(off, quarter)], maskv.at[m], mask_sems.at[m])
        mc.start()
        mask_copies[m] = mc

    barrier = pltpu.get_barrier_semaphore()
    for dev in (dev_d, dev_x, dev_xd, dev_y, *dev_z):
        pl.semaphore_signal(barrier, inc=1, device_id=dev, device_id_type=MESH)
    pl.semaphore_wait(barrier, 7)

    y_off = pl.multiple_of(y * own_users, own_users)
    u0_y = cp.send(u0_ref, upan.at[0, :, pl.ds(y_off, own_users)], dev_y)
    upan[0, :, pl.ds(y_off, own_users)] = u0_ref[...]
    i0_x = cp.send(i0_ref, ipan.at[0, 2], dev_x)
    i0_d = cp.send(i0_ref, ipan.at[0, 1], dev_d)
    ipan[0, 0] = i0_ref[...]

    racc[...] = jnp.zeros_like(racc)

    def sums(m):
        def body(j, carry):
            off = pl.multiple_of(j * LB, LB)
            part = maskv[m, pl.ds(0, 8), pl.ds(off, LB)]
            for i in range(1, users // 8):
                part = part + maskv[m, pl.ds(8 * i, 8), pl.ds(off, LB)]
            csum[m, :, pl.ds(off, LB)] = jnp.sum(part.astype(F32), axis=0, keepdims=True)
            row = maskv[m, :, pl.ds(off, 128)]
            for g in range(1, LB // 128):
                row = row + maskv[m, :, pl.ds(pl.multiple_of(off + 128 * g, 128), 128)]
            racc[...] += row
            return carry
        lax.fori_loop(0, quarter // LB, body, 0)

    def one_hots(m):
        base = pl.multiple_of(rel(m) * home, home)
        for row, oh, hi in ((1, ohp, hip), (2, ohn, hin)):
            ids = trip_ref[pl.ds(row, 1), pl.ds(base, home)]
            owned = ids // quarter == y * NQ + r
            hi[m] = (ids % quarter) // GL
            low = jnp.where(owned, ids % GL, -1)
            for t in range(home // LB):
                lanes = low[:, t * LB:(t + 1) * LB]
                hit = lax.broadcasted_iota(jnp.int32, (GL, LB), 0) == lanes
                oh[m, :, t * LB:(t + 1) * LB] = jnp.where(hit, 1.0, 0.0).astype(BF16)

    csum_d, csum_x = {}, {}
    i0_f = None
    prev = None

    def chip_sums(m):
        csum_d[m].wait_recv()
        cch[m] = csum[m] + crd[m]
        csum_x[m ^ 2] = cp.send(cch.at[m], crx.at[m ^ 2], dev_x)

    for m in (3, 2, 1, 0):
        mask_copies[m].wait()
        sums(m)
        csum_d[m ^ 1] = cp.send(csum.at[m], crd.at[m ^ 1], dev_d)
        if m == 2:
            i0_x.wait_recv()
            i0_f = cp.send(ipan.at[0, 2], ipan.at[0, 3], dev_d)
            chip_sums(3)
            chip_sums(2)
    rows = jnp.transpose(racc[...].astype(F32), (1, 0))
    rsum[...] = jnp.sum(rows, axis=0, keepdims=True)
    rs_y = cp.send(rsum, rrecv, dev_y)
    chip_sums(1)
    chip_sums(0)

    rs_y.wait_recv()
    inv_row = lax.rsqrt(jnp.maximum(rsum[...] + rrecv[...], 1.0))
    invu[...] = jnp.transpose(jnp.broadcast_to(inv_row, (128, users)), (1, 0))
    u0_y.wait_recv()

    def build(m, s):
        def body(j, carry):
            iu = invu[...]
            for g in range(LB // 128):
                off = pl.multiple_of(s * sc + j * LB + g * 128, 128)
                blk = maskv[m, :, pl.ds(off, 128)]
                ii = invi[m, :, pl.ds(off, 128)]
                adj[m, :, pl.ds(off, 128)] = jnp.where(blk != 0, iu * ii, 0.0).astype(BF16)
            return carry
        lax.fori_loop(0, sc // LB, body, 0)

    def item_piece(k, m, s):
        sl = pl.ds(s * sc, sc)
        ipart[k, m, :, sl] = jnp.dot(upan[k], adj[m, :, sl], preferred_element_type=F32)

    def user_part(k, m):
        return lax.dot_general(ipan[k, m], adj[m], (((1,), (1,)), ((), ())), preferred_element_type=F32)

    def to_core(k, m, s):
        sl = pl.ds(s * sc, sc)
        return cp.send(ipart.at[k, m, :, sl], ird.at[k, (m ^ 1) // 2, :, sl], dev_d)

    def to_x(k, s, got):
        sl = pl.ds(s * sc, sc)
        got.wait_recv()
        isum[k, :, sl] = ipart[k, 2, :, sl] + ird[k, 1, :, sl]
        return cp.send(isum.at[k, :, sl], irx.at[k, :, sl], dev_x)

    def own_piece(k, s, got_d, got_x):
        sl = pl.ds(s * sc, sc)
        got_d.wait_recv()
        got_x.wait_recv()
        total = (ipart[k, 0, :, sl] + ird[k, 0, :, sl]) + irx[k, :, sl]
        ipan[k + 1, 0, :, sl] = total.astype(BF16)

    def gather_piece(k, s):
        sl = pl.ds(s * sc, sc)
        gx = cp.send(ipan.at[k, 0, :, sl], ipan.at[k, 2, :, sl], dev_x)
        gd = cp.send(ipan.at[k, 0, :, sl], ipan.at[k, 1, :, sl], dev_d)
        return gx, gd

    def forward_piece(k, s, gx):
        sl = pl.ds(s * sc, sc)
        gx.wait_recv()
        return cp.send(ipan.at[k, 2, :, sl], ipan.at[k, 3, :, sl], dev_d)

    def send_user(k, acc):
        upart[k] = acc
        return cp.send(upart.at[k], urecv.at[k], dev_y)

    def take_user(k, got):
        got.wait_recv()
        upan[k + 1] = (upart[k] + urecv[k]).astype(BF16)

    d1, x1 = {}, {}
    for m in (3, 2, 1, 0):
        csum_x[m].wait_recv()
        invi[m] = lax.rsqrt(jnp.maximum(cch[m] + crx[m], 1.0))
        for s in range(NS):
            build(m, s)
            item_piece(0, m, s)
            if m in (3, 1):
                d1[m ^ 1, s] = to_core(0, m, s)
            if m == 2:
                x1[s] = to_x(0, s, d1[2, s])
    i0_d.wait_recv()
    i0_f.wait_recv()
    acc = user_part(0, 0)
    for m in (1, 2, 3):
        acc = acc + user_part(0, m)
    u1 = send_user(0, acc)
    for m in (3, 2, 1, 0):
        one_hots(m)
    ubase = pl.multiple_of(r * home, home)
    uids = trip_ref[pl.ds(0, 1), pl.ds(ubase, home)]
    urow = uids // users
    hiu[...] = urow
    for t in range(home // LB):
        lanes = (uids % users)[:, t * LB:(t + 1) * LB]
        hit = lax.broadcasted_iota(jnp.int32, (GL, LB), 0) == lanes
        ohu[:, t * LB:(t + 1) * LB] = jnp.where(hit, 1.0, 0.0).astype(BF16)

    take_user(0, u1)
    d2, x2 = {}, {}
    for m in (3, 2, 1, 0):
        for s in range(NS):
            item_piece(1, m, s)
            if m in (3, 1):
                d2[m ^ 1, s] = to_core(1, m, s)
    g1 = {}
    for s in range(NS):
        own_piece(0, s, d1[0, s], x1[s])
        g1[s] = gather_piece(1, s)
    for s in range(NS):
        x2[s] = to_x(1, s, d2[2, s])
    f1 = {}
    for s in range(NS):
        f1[s] = forward_piece(1, s, g1[s][0])
    acc = user_part(1, 0)
    for s in range(NS):
        g1[s][1].wait_recv()
    acc = acc + user_part(1, 1)
    acc = acc + user_part(1, 2)
    for s in range(NS):
        f1[s].wait_recv()
    acc = acc + user_part(1, 3)
    u2 = send_user(1, acc)
    g2 = {}
    take_user(1, u2)
    d3, x3 = {}, {}
    for m in (3, 2, 1, 0):
        for s in range(NS):
            item_piece(2, m, s)
            if m in (3, 1):
                d3[m ^ 1, s] = to_core(2, m, s)
            if m == 2:
                x3[s] = to_x(2, s, d3[2, s])
    for s in range(NS):
        own_piece(1, s, d2[0, s], x2[s])
        g2[s] = gather_piece(2, s)
    f2 = {}
    for s in range(NS):
        f2[s] = forward_piece(2, s, g2[s][0])
    acc = user_part(2, 0)
    for s in range(NS):
        g2[s][1].wait_recv()
    acc = acc + user_part(2, 1)
    acc = acc + user_part(2, 2)
    for s in range(NS):
        f2[s].wait_recv()
    acc = acc + user_part(2, 3)
    u3 = send_user(2, acc)

    for s in range(NS):
        own_piece(2, s, d3[0, s], x3[s])
        sl = pl.ds(s * sc, sc)
        tot = ((ipan[0, 0, :, sl].astype(F32) + ipan[1, 0, :, sl].astype(F32))
               + ipan[2, 0, :, sl].astype(F32)) + ipan[3, 0, :, sl].astype(F32)
        outi_ref[:, sl] = (tot * (1.0 / (NUM_LAYERS + 1))).astype(BF16)
    table = jnp.concatenate(
        [outi_ref[:, g * GL:(g + 1) * GL] for g in range(quarter // GL)], axis=0)

    def pick(tab, oh, hi, n):
        got = jnp.dot(tab, oh, preferred_element_type=F32)
        rows16 = got.shape[0] // n
        out = jnp.where(hi == 0, got[:rows16], 0.0)
        for g in range(1, n):
            out = out + jnp.where(hi == g, got[g * rows16:(g + 1) * rows16], 0.0)
        return out

    def differences(m):
        for t in range(home // LB):
            sl = slice(t * LB, (t + 1) * LB)
            pos = pick(table, ohp[m, :, sl], hip[m, :, sl], quarter // GL)
            neg = pick(table, ohn[m, :, sl], hin[m, :, sl], quarter // GL)
            gpart[m, :, sl] = pos - neg

    differences(3)
    gd3 = cp.send(gpart.at[3], grd.at[1], dev_d)
    differences(2)
    gd3.wait_recv()
    gsum[1] = gpart[2] + grd[1]
    gx = cp.send(gsum.at[1], grx, dev_x)
    differences(1)
    gd1 = cp.send(gpart.at[1], grd.at[0], dev_d)
    differences(0)

    take_user(2, u3)
    ut = ((upan[0].astype(F32) + upan[1].astype(F32)) + upan[2].astype(F32)) + upan[3].astype(F32)
    eu[0] = (ut * (1.0 / (NUM_LAYERS + 1))).astype(BF16)
    outu_ref[...] = eu[0, :, pl.ds(y_off, own_users)]
    e1 = cp.send(eu.at[0], eu.at[1], dev_d)
    e2 = cp.send(eu.at[0], eu.at[2], dev_x)
    e3 = cp.send(eu.at[0], eu.at[3], dev_xd)

    gd1.wait_recv()
    gx.wait_recv()
    gsum[0] = (gpart[0] + grd[0]) + grx[...]
    gy = cp.send(gsum.at[0], gry, dev_y)

    e1.wait_recv()
    e2.wait_recv()
    e3.wait_recv()
    utab = jnp.concatenate([eu[m] for m in range(NQ)], axis=0)
    blk_id = hiu[...]
    place = jnp.where(blk_id // 2 == x, 0, 2) + jnp.where(blk_id % 2 == c, 0, 1)
    picked = []
    for t in range(home // LB):
        sl = slice(t * LB, (t + 1) * LB)
        picked.append(pick(utab, ohu[:, sl], place[:, sl], NQ))
    gy.wait_recv()
    for t in range(home // LB):
        sl = slice(t * LB, (t + 1) * LB)
        diff = gsum[0, :, sl] + gry[:, sl]
        zbuf[z, :, sl] = jnp.sum(picked[t] * diff, axis=0, keepdims=True)
    zc = [cp.send(zbuf.at[z], zbuf.at[z], dev) for dev in dev_z]
    for copy in zc:
        copy.wait_recv()
    score = ((zbuf[0] + zbuf[1]) + zbuf[2]) + zbuf[3]
    neg = -score
    lossb[r] = jnp.maximum(neg, 0.0) + jnp.log1p(jnp.exp(-jnp.abs(neg)))
    lc = [cp.send(lossb.at[r], lossb.at[r], dev) for dev in (dev_d, dev_x, dev_xd)]
    for copy in lc:
        copy.wait_recv()
    loss_ref[...] = lossb[...]
    cp.drain()


def solution(mesh):
    def local_fn(mask_blk, user_sh, item_sh, triples):
        users, items = mask_blk.shape
        cols, own_users = user_sh.shape[1], user_sh.shape[0]
        quarter = items // NQ
        home = triples.shape[0] // NQ
        vm = pltpu.VMEM
        nl = NUM_LAYERS
        scratch = [
            vm((NQ, users, quarter), jnp.int32), vm((NQ, users, quarter), BF16),
            vm((NQ, 1, quarter), F32), vm((NQ, 1, quarter), F32), vm((NQ, 1, quarter), F32),
            vm((NQ, 1, quarter), F32), vm((NQ, 1, quarter), F32),
            vm((users, 128), jnp.int32), vm((1, users), F32), vm((1, users), F32), vm((users, 128), F32),
            vm((nl + 1, cols, users), BF16), vm((nl, cols, users), F32), vm((nl, cols, users), F32),
            vm((nl + 1, NQ, cols, quarter), BF16), vm((nl, NQ, cols, quarter), F32),
            vm((nl, 2, cols, quarter), F32), vm((nl, cols, quarter), F32), vm((nl, cols, quarter), F32),
            vm((NQ, GL, home), BF16), vm((NQ, GL, home), BF16), vm((GL, home), BF16),
            vm((NQ, 1, home), jnp.int32), vm((NQ, 1, home), jnp.int32), vm((1, home), jnp.int32),
            vm((NQ, cols, home), F32), vm((2, cols, home), F32), vm((2, cols, home), F32),
            vm((cols, home), F32), vm((cols, home), F32),
            vm((NQ, cols, users), BF16), vm((4, 1, home), F32), vm((NQ, 1, home), F32),
            pltpu.SemaphoreType.DMA((NQ,)),
            pltpu.SemaphoreType.DMA((NUM_SEMS,)), pltpu.SemaphoreType.DMA((NUM_SEMS,)),
        ]
        vspec = pl.BlockSpec(memory_space=pltpu.VMEM)
        out_u, out_i, loss = pl.pallas_call(
            kernel,
            out_shape=[
                jax.ShapeDtypeStruct((cols, own_users), BF16),
                jax.ShapeDtypeStruct((cols, quarter), BF16),
                jax.ShapeDtypeStruct((NQ, 1, home), F32)],
            in_specs=[pl.BlockSpec(memory_space=pl.ANY), vspec, vspec, vspec],
            out_specs=[vspec, vspec, vspec],
            scratch_shapes=scratch,
            compiler_params=pltpu.CompilerParams(
                collective_id=0, has_side_effects=True, vmem_limit_bytes=60 * 1024 * 1024),
        )(mask_blk, user_sh.T, item_sh.T, triples.T)
        return out_u.T, out_i.T, loss.reshape(-1)

    return jax.shard_map(
        local_fn, mesh=mesh,
        in_specs=(P("row", "col"), P(("row", "col"), "emb"), P(("col", "row"), "emb"), P()),
        out_specs=(P(("row", "col"), "emb"), P(("col", "row"), "emb"), P()),
        check_vma=False)
```

time: 334 us -> 84.7 us (0.25)
  waiting for transfers between devices: 147 us -> 0 us
  Pallas kernels: 0 us -> 79.7 us
  blocking collectives: 58.1 us -> 0 us
  local copies, waits for them, and re-layouts: 47.1 us -> 4.15 us
  other arithmetic: 34.3 us -> 0 us
  matrix products: 32.3 us -> 0 us
  between operations: 14.3 us -> 0.64 us
    pallas_call x0 -> x1, Pallas kernels: none -> 79.7 us  [local_fn(): pl.pallas_call(kernel, out_shape=[jax.ShapeDtypeStruct((cols, own_users),...]
    reduce_scatter x6 -> x0, waiting for transfers between devices: 73.7 us -> none  [the longest x3 64.5 us: local_fn(): lax.psum_scatter(item_part, 'row', scatter_dimension=0, tiled=True)]
    psum x2 -> x0, waiting for transfers between devices: 72.7 us -> none  [the longest x1 55.9 us: bpr_terms(): fetched = lax.psum(fetched, ('row', 'col'))]
    gather x3 -> x0, local copies, waits for them, and re-layouts: 39.2 us -> none  [lookup_rows(): picked = jnp.take(table, jnp.clip(local_ids, 0, own_rows - 1), axis=0)]
    all_gather x6 -> x0, blocking collectives: 34.1 us -> none  [the longest x3 20.9 us: local_fn(): item_panel = lax.all_gather(item_cur, 'row', axis=0, tiled=True)]
    dot_general x6 -> x0, matrix products: 32.3 us -> none  [the longest x3 16.9 us: local_fn(): lax.dot_general(adj_blk, user_panel, (((0,), (0,)), ((), ())), preferred_...]
    psum x2 -> x0, blocking collectives: 24 us -> none  [the longest x1 18.7 us: bpr_terms(): score = lax.psum(jnp.sum(e_user * (e_pos - e_neg), axis=1), 'emb')]
    convert_element_type x6 -> x0, other arithmetic: 11.3 us -> none  [the longest x1 7.11 us: norm_adjacency(): (inv_user[:, None] * mask_blk.astype(jnp.float32) * inv_item[None, :]).as...]
  transfers between devices with their start and end apart: 8 -> 0, of which waited for: 7 -> 0; matrix products, arithmetic and copies ran while one was open for 17% -> 0% of each run, Pallas kernels for 0% -> 0%
where the time goes in v1:
time: 84.7 us; the launch traced here: 84.4 us
  Pallas kernels  79.7 us (94%)
  local copies, waits for them, and re-layouts  4.15 us (5%)
    pallas_call x1, Pallas kernels, local_fn(): pl.pallas_call(kernel, out_shape=[jax.ShapeDtypeStruct((cols, own_users),...  79.7 us
    unnamed x3, local copies, waits for them, and re-layouts  4.15 us

profile of v1, /device:TPU:0, one launch (start us, length us, event | category | flops | bytes accessed | tf_op | source)
XLA Modules:
  0.0 84.4 jit_solution(1591591612921503163)
XLA Ops:
  0.6 79.7 %shard_map.67 = (bf16[16,128]{1,0:T(8,128)(2,1)}, bf16[16,4096]{1,0:T(8,128)(2,1)}, f32[4,1,1024]{2,1,0:T(1,128)}) custom-call(s32[256,16384]{1,0:T(8,128)} %mask_hbm.1, bf16[16,128]{1,0:T(8,128)(2,1)} %bitcast.10, bf16[16,4096]{1,0:T(8,128)(2,1)} %bitcast.6, s32[3,4096]{1,0:T(4,128)} %bitcast.8), custom_call_target="tpu_custom_call" | custom-call | tf_op jit(solution)/shard_map/pallas_call | solution.py:382
  80.3 1.3 %copy.10 = bf16[128,16]{0,1:T(8,128)(2,1)} copy(bf16[128,16]{0,1:T(8,128)(2,1)} %bitcast.11) | data formatting | bytes 8192
  81.6 1.6 %copy.11 = bf16[4096,16]{0,1:T(8,128)(2,1)} copy(bf16[4096,16]{0,1:T(8,128)(2,1)} %bitcast.7) | data formatting | bytes 262144
  83.1 1.3 %copy.12 = f32[4096]{0:T(1024)} copy(f32[4096]{0:T(1024)} %bitcast.9) | data formatting | bytes 32768

commit v2 on v1

v2 whole, which is shorter than its diff:
```python
import functools

import jax
import jax.numpy as jnp
from jax import lax
from jax.experimental import pallas as pl
from jax.experimental.pallas import tpu as pltpu
from jax.sharding import PartitionSpec as P

NUM_LAYERS = 3
MESH = pl.DeviceIdType.MESH
F32 = jnp.float32
BF16 = jnp.bfloat16

NQ = 4
NS = 4
LB = 256
GL = 256


class Copies:
    def __init__(self, send_sems, recv_sems):
        self.send_sems, self.recv_sems, self.started = send_sems, recv_sems, []

    def send(self, src, dst, device):
        k = len(self.started)
        copy = pltpu.make_async_remote_copy(
            src_ref=src, dst_ref=dst, send_sem=self.send_sems.at[k],
            recv_sem=self.recv_sems.at[k], device_id=device, device_id_type=MESH)
        copy.start()
        self.started.append(copy)
        return copy

    def drain(self):
        for copy in self.started:
            copy.wait_send()


NUM_SEMS = 120


class Phase:
    def __init__(self):
        self.current = None

    def __call__(self, name):
        if self.current is not None:
            self.current.__exit__(None, None, None)
        self.current = None
        if name:
            self.current = jax.named_scope(name)
            self.current.__enter__()


def kernel(mask_hbm, u0_hbm, i0_hbm, trip_hbm, outu_ref, outi_ref, loss_ref,
           maskv, adj, csum, crd, crx, cch, invi, racc, rsum, rrecv, invu, trip_ref,
           upan, upart, urecv, ipan, ipart, ird, irx, isum,
           ohp, ohn, ohu, hip, hin, hiu, gpart, gsum, grd, grx, gry, eu, zbuf, lossb,
           in_sems, send_sems, recv_sems):
    users = maskv.shape[1]
    quarter = maskv.shape[2]
    own_users = u0_hbm.shape[1]
    sc = quarter // NS
    home = ohp.shape[2]
    hh = home // 2

    z = lax.axis_index("emb")
    y = lax.axis_index("col")
    r = lax.axis_index("row")
    x = r // 2
    c = r % 2
    nz = 4

    def rel(m):
        xx = x if m < 2 else 1 - x
        cc = c if m % 2 == 0 else 1 - c
        return 2 * xx + cc

    dev_d = (z, y, rel(1))
    dev_x = (z, y, rel(2))
    dev_xd = (z, y, rel(3))
    dev_y = (z, 1 - y, r)
    dev_z = [((z + k) % nz, y, r) for k in (1, 2, 3)]

    cp = Copies(send_sems, recv_sems)
    phase = Phase()
    phase("start")

    def load(src, dst, k):
        copy = pltpu.make_async_copy(src, dst, in_sems.at[k])
        copy.start()
        return copy

    y_off = pl.multiple_of(y * own_users, own_users)
    mask_copies = {}
    for m in (3, 2, 1, 0):
        off = pl.multiple_of(rel(m) * quarter, quarter)
        mask_copies[m] = load(mask_hbm.at[:, pl.ds(off, quarter)], maskv.at[m], m)
        if m == 3:
            u0_in = load(u0_hbm, upan.at[0, :, pl.ds(y_off, own_users)], 4)
            i0_in = load(i0_hbm, ipan.at[0, 0], 5)
            trip_in = load(trip_hbm, trip_ref, 6)

    barrier = pltpu.get_barrier_semaphore()
    for dev in (dev_d, dev_x, dev_xd, dev_y, *dev_z):
        pl.semaphore_signal(barrier, inc=1, device_id=dev, device_id_type=MESH)

    racc[...] = jnp.zeros_like(racc)

    def sums(m):
        def body(j, carry):
            off = pl.multiple_of(j * LB, LB)
            part = None
            for i in range(users // 16):
                rows = pl.ds(16 * i, 16)
                blk = maskv[m, rows, pl.ds(off, LB)]
                adj[m, rows, pl.ds(off, LB)] = blk.astype(F32).astype(BF16)
                two = blk[:8] + blk[8:]
                part = two if part is None else part + two
                row = blk[:, :128]
                for g in range(1, LB // 128):
                    row = row + blk[:, 128 * g:128 * (g + 1)]
                racc[rows, :] += row
            csum[m, :, pl.ds(off, LB)] = jnp.sum(part.astype(F32), axis=0, keepdims=True)
            return carry
        lax.fori_loop(0, quarter // LB, body, 0)

    def one_hots(m):
        base = pl.multiple_of(rel(m) * home, home)
        for row, oh, hi in ((1, ohp, hip), (2, ohn, hin)):
            ids = trip_ref[pl.ds(row, 1), pl.ds(base, home)]
            owned = ids // quarter == y * NQ + r
            hi[m] = (ids % quarter) // GL
            low = jnp.where(owned, ids % GL, -1)
            for t in range(home // LB):
                lanes = low[:, t * LB:(t + 1) * LB]
                hit = lax.broadcasted_iota(jnp.int32, (GL, LB), 0) == lanes
                oh[m, :, t * LB:(t + 1) * LB] = jnp.where(hit, 1.0, 0.0).astype(BF16)

    def user_one_hots():
        base = pl.multiple_of(r * home, home)
        uids = trip_ref[pl.ds(0, 1), pl.ds(base, home)]
        hiu[...] = uids // users
        for t in range(home // LB):
            lanes = (uids % users)[:, t * LB:(t + 1) * LB]
            hit = lax.broadcasted_iota(jnp.int32, (GL, LB), 0) == lanes
            ohu[:, t * LB:(t + 1) * LB] = jnp.where(hit, 1.0, 0.0).astype(BF16)

    csum_d, csum_x = {}, {}

    def chip_sums(m):
        csum_d[m].wait_recv()
        cch[m] = csum[m] + crd[m]
        csum_x[m ^ 2] = cp.send(cch.at[m], crx.at[m ^ 2], dev_x)

    def send_sums(m):
        csum_d[m ^ 1] = cp.send(csum.at[m], crd.at[m ^ 1], dev_d)

    for m in (3, 2):
        phase(f"mask_wait{m}")
        mask_copies[m].wait()
        phase(f"sums{m}")
        sums(m)
    phase("in_wait")
    u0_in.wait()
    i0_in.wait()
    trip_in.wait()
    phase("barrier")
    pl.semaphore_wait(barrier, 7)
    phase("layer0")
    send_sums(3)
    send_sums(2)
    u0_y = cp.send(upan.at[0, :, pl.ds(y_off, own_users)], upan.at[0, :, pl.ds(y_off, own_users)], dev_y)
    i0_x = cp.send(ipan.at[0, 0], ipan.at[0, 2], dev_x)
    i0_d = cp.send(ipan.at[0, 0], ipan.at[0, 1], dev_d)
    for m in (1, 0):
        phase(f"mask_wait{m}")
        mask_copies[m].wait()
        phase(f"sums{m}")
        sums(m)
        send_sums(m)
        if m == 1:
            phase("chip32")
            chip_sums(3)
            chip_sums(2)
    phase("rows")
    rows = jnp.transpose(racc[...].astype(F32), (1, 0))
    rsum[...] = jnp.sum(rows, axis=0, keepdims=True)
    rs_y = cp.send(rsum, rrecv, dev_y)
    one_hots(3)
    one_hots(2)
    phase("chip10")
    chip_sums(1)
    chip_sums(0)
    phase("onehots")
    one_hots(1)
    one_hots(0)
    user_one_hots()
    phase("i0_x_wait")
    i0_x.wait_recv()
    i0_f = cp.send(ipan.at[0, 2], ipan.at[0, 3], dev_d)
    u0_y.wait_recv()
    phase("rs_wait")
    rs_y.wait_recv()
    phase("invu")
    inv_row = lax.rsqrt(jnp.maximum(rsum[...] + rrecv[...], 1.0))
    invu[...] = jnp.transpose(jnp.broadcast_to(inv_row, (128, users)), (1, 0))
    phase("cx_wait")
    for m in (3, 2, 1, 0):
        csum_x[m].wait_recv()
        invi[m] = lax.rsqrt(jnp.maximum(cch[m] + crx[m], 1.0))

    def build(m, s):
        def body(j, carry):
            off = pl.multiple_of(s * sc + j * LB, LB)
            ii = invi[m, :, pl.ds(off, LB)]
            for i in range(users // 16):
                rows = pl.ds(16 * i, 16)
                iu = invu[rows, :]
                for g in range(LB // 128):
                    lanes = pl.ds(pl.multiple_of(off + 128 * g, 128), 128)
                    scale = (iu * ii[:, 128 * g:128 * (g + 1)]).astype(BF16)
                    adj[m, rows, lanes] = scale * adj[m, rows, lanes]
            return carry
        lax.fori_loop(0, sc // LB, body, 0)

    def item_piece(k, m, s):
        sl = pl.ds(s * sc, sc)
        ipart[k, m, :, sl] = jnp.dot(upan[k], adj[m, :, sl], preferred_element_type=F32)

    def user_part(k, m):
        return lax.dot_general(adj[m], ipan[k, m], (((1,), (1,)), ((), ())), preferred_element_type=F32)

    def to_core(k, m, s):
        sl = pl.ds(s * sc, sc)
        return cp.send(ipart.at[k, m, :, sl], ird.at[k, (m ^ 1) // 2, :, sl], dev_d)

    def to_x(k, s, got):
        sl = pl.ds(s * sc, sc)
        got.wait_recv()
        isum[k, :, sl] = ipart[k, 2, :, sl] + ird[k, 1, :, sl]
        return cp.send(isum.at[k, :, sl], irx.at[k, :, sl], dev_x)

    def own_piece(k, s, got_d, got_x):
        sl = pl.ds(s * sc, sc)
        got_d.wait_recv()
        got_x.wait_recv()
        total = (ipart[k, 0, :, sl] + ird[k, 0, :, sl]) + irx[k, :, sl]
        ipan[k + 1, 0, :, sl] = total.astype(BF16)

    def gather_piece(k, s):
        sl = pl.ds(s * sc, sc)
        gx = cp.send(ipan.at[k, 0, :, sl], ipan.at[k, 2, :, sl], dev_x)
        gd = cp.send(ipan.at[k, 0, :, sl], ipan.at[k, 1, :, sl], dev_d)
        return gx, gd

    def forward_piece(k, s, gx):
        sl = pl.ds(s * sc, sc)
        gx.wait_recv()
        return cp.send(ipan.at[k, 2, :, sl], ipan.at[k, 3, :, sl], dev_d)

    def send_user(k, acc):
        upart[k] = jnp.transpose(acc, (1, 0))
        return cp.send(upart.at[k], urecv.at[k], dev_y)

    def take_user(k, got):
        got.wait_recv()
        upan[k + 1] = (upart[k] + urecv[k]).astype(BF16)

    d, xs = [{}, {}, {}], [{}, {}, {}]
    g, f = {}, {}
    phase("build32")
    for s in range(NS):
        build(3, s)
        item_piece(0, 3, s)
        d[0][2, s] = to_core(0, 3, s)
        build(2, s)
        item_piece(0, 2, s)
        if s:
            xs[0][s - 1] = to_x(0, s - 1, d[0][2, s - 1])
    xs[0][NS - 1] = to_x(0, NS - 1, d[0][2, NS - 1])
    phase("upart0_32")
    i0_d.wait_recv()
    i0_f.wait_recv()
    acc = user_part(0, 3) + user_part(0, 2)
    phase("build10")
    for s in range(NS):
        build(1, s)
        item_piece(0, 1, s)
        d[0][0, s] = to_core(0, 1, s)
        build(0, s)
        item_piece(0, 0, s)

    def own_gather(k, s):
        own_piece(k, s, d[k][0, s], xs[k][s])
        g[k + 1, s] = gather_piece(k + 1, s)

    phase("own1_0")
    own_gather(0, 0)
    phase("upart0_1")
    acc = acc + user_part(0, 1)
    phase("own1_1")
    own_gather(0, 1)
    phase("upart0_0")
    acc = acc + user_part(0, 0)
    u1 = send_user(0, acc)
    phase("own1_2")
    own_gather(0, 2)
    phase("own1_3")
    own_gather(0, 3)
    phase("upart1_0")
    acc = user_part(1, 0)
    phase("upart1_1")
    for s in range(NS):
        g[1, s][1].wait_recv()
    acc = acc + user_part(1, 1)
    phase("u1_wait")
    take_user(0, u1)
    phase("items2_32")
    for s in range(NS):
        item_piece(1, 3, s)
        d[1][2, s] = to_core(1, 3, s)
        item_piece(1, 2, s)
        if s:
            xs[1][s - 1] = to_x(1, s - 1, d[1][2, s - 1])
        if s == 1:
            f[1, 0] = forward_piece(1, 0, g[1, 0][0])
        if s == 2:
            f[1, 1] = forward_piece(1, 1, g[1, 1][0])
    xs[1][NS - 1] = to_x(1, NS - 1, d[1][2, NS - 1])
    phase("fwd1")
    f[1, 2] = forward_piece(1, 2, g[1, 2][0])
    f[1, 3] = forward_piece(1, 3, g[1, 3][0])
    phase("upart1_2")
    acc = acc + user_part(1, 2)
    phase("f1_wait")
    for s in range(NS):
        f[1, s].wait_recv()
    phase("upart1_3")
    acc = acc + user_part(1, 3)
    u2 = send_user(1, acc)
    phase("items2_10")
    for s in range(NS):
        item_piece(1, 1, s)
        d[1][0, s] = to_core(1, 1, s)
        item_piece(1, 0, s)
    phase("u2_wait")
    take_user(1, u2)
    phase("items3_32")
    for s in range(NS):
        item_piece(2, 3, s)
        d[2][2, s] = to_core(2, 3, s)
        item_piece(2, 2, s)
        if s:
            xs[2][s - 1] = to_x(2, s - 1, d[2][2, s - 1])
    xs[2][NS - 1] = to_x(2, NS - 1, d[2][2, NS - 1])
    phase("own2")
    for s in range(NS):
        own_gather(1, s)
    phase("items3_10")
    for s in range(NS):
        item_piece(2, 1, s)
        d[2][0, s] = to_core(2, 1, s)
        item_piece(2, 0, s)
    phase("upart2_01")
    acc = user_part(2, 0)
    for s in range(NS):
        g[2, s][1].wait_recv()
    acc = acc + user_part(2, 1)

    phase("own3")
    for s in range(NS):
        own_piece(2, s, d[2][0, s], xs[2][s])
        sl = pl.ds(s * sc, sc)
        tot = ((ipan[0, 0, :, sl].astype(F32) + ipan[1, 0, :, sl].astype(F32))
               + ipan[2, 0, :, sl].astype(F32)) + ipan[3, 0, :, sl].astype(F32)
        outi_ref[:, sl] = (tot * (1.0 / (NUM_LAYERS + 1))).astype(BF16)
    phase("table")
    table = jnp.concatenate(
        [outi_ref[:, g0 * GL:(g0 + 1) * GL] for g0 in range(quarter // GL)], axis=0)

    def pick(tab, oh, hi, n):
        got = jnp.dot(tab, oh, preferred_element_type=F32)
        rows16 = got.shape[0] // n
        out = jnp.where(hi == 0, got[:rows16], 0.0)
        for g0 in range(1, n):
            out = out + jnp.where(hi == g0, got[g0 * rows16:(g0 + 1) * rows16], 0.0)
        return out

    def differences(m, h):
        for t in range(hh // LB):
            sl = slice(h * hh + t * LB, h * hh + (t + 1) * LB)
            pos = pick(table, ohp[m, :, sl], hip[m, :, sl], quarter // GL)
            neg = pick(table, ohn[m, :, sl], hin[m, :, sl], quarter // GL)
            gpart[m, :, sl] = pos - neg

    half = [pl.ds(0, hh), pl.ds(hh, hh)]
    gd3, gd1, gx, gy = {}, {}, {}, {}
    phase("diff3")
    for h in (0, 1):
        differences(3, h)
        gd3[h] = cp.send(gpart.at[3, :, half[h]], grd.at[1, :, half[h]], dev_d)
    phase("diff2")
    for h in (0, 1):
        differences(2, h)
        gd3[h].wait_recv()
        gsum[1, :, half[h]] = gpart[2, :, half[h]] + grd[1, :, half[h]]
        gx[h] = cp.send(gsum.at[1, :, half[h]], grx.at[:, half[h]], dev_x)
    phase("diff1")
    for h in (0, 1):
        differences(1, h)
        gd1[h] = cp.send(gpart.at[1, :, half[h]], grd.at[0, :, half[h]], dev_d)
    phase("fwd2")
    for s in range(NS):
        f[2, s] = forward_piece(2, s, g[2, s][0])
    phase("upart2_2")
    acc = acc + user_part(2, 2)
    phase("f2_wait")
    for s in range(NS):
        f[2, s].wait_recv()
    phase("upart2_3")
    acc = acc + user_part(2, 3)
    u3 = send_user(2, acc)
    phase("diff0")
    for h in (0, 1):
        differences(0, h)
    phase("g_wait")
    for h in (0, 1):
        gd1[h].wait_recv()
        gx[h].wait_recv()
        gsum[0, :, half[h]] = (gpart[0, :, half[h]] + grd[0, :, half[h]]) + grx[:, half[h]]
        gy[h] = cp.send(gsum.at[0, :, half[h]], gry.at[:, half[h]], dev_y)

    phase("u3_wait")
    take_user(2, u3)
    phase("finalu")
    ut = ((upan[0].astype(F32) + upan[1].astype(F32)) + upan[2].astype(F32)) + upan[3].astype(F32)
    eu[0] = (ut * (1.0 / (NUM_LAYERS + 1))).astype(BF16)
    e1 = cp.send(eu.at[0], eu.at[1], dev_d)
    e2 = cp.send(eu.at[0], eu.at[2], dev_x)
    e3 = cp.send(eu.at[0], eu.at[3], dev_xd)
    outu_ref[...] = eu[0, :, pl.ds(y_off, own_users)]

    phase("e_wait")
    e1.wait_recv()
    e2.wait_recv()
    e3.wait_recv()
    phase("picku")
    utab = jnp.concatenate([eu[m] for m in range(NQ)], axis=0)
    blk_id = hiu[...]
    place = jnp.where(blk_id // 2 == x, 0, 2) + jnp.where(blk_id % 2 == c, 0, 1)
    picked = []
    for t in range(home // LB):
        sl = slice(t * LB, (t + 1) * LB)
        picked.append(pick(utab, ohu[:, sl], place[:, sl], NQ))
    phase("gy_wait")
    gy[0].wait_recv()
    gy[1].wait_recv()
    phase("dot")
    for t in range(home // LB):
        sl = slice(t * LB, (t + 1) * LB)
        diff = gsum[0, :, sl] + gry[:, sl]
        zbuf[z, :, sl] = jnp.sum(picked[t] * diff, axis=0, keepdims=True)
    zc = [cp.send(zbuf.at[z], zbuf.at[z], dev) for dev in dev_z]
    phase("z_wait")
    for copy in zc:
        copy.wait_recv()
    phase("loss")
    score = ((zbuf[0] + zbuf[1]) + zbuf[2]) + zbuf[3]
    neg = -score
    lossb[r] = jnp.maximum(neg, 0.0) + jnp.log1p(jnp.exp(-jnp.abs(neg)))
    lc = [cp.send(lossb.at[r], lossb.at[r], dev) for dev in (dev_d, dev_x, dev_xd)]
    phase("loss_wait")
    for copy in lc:
        copy.wait_recv()
    phase("end")
    loss_ref[...] = lossb[...]
    phase("drain")
    cp.drain()
    phase(None)


def emit(u_in, i_in, l_in, u_out, i_out, l_out):
    u_out[...] = u_in[...]
    i_out[...] = i_in[...]
    l_out[...] = l_in[...]


def solution(mesh):
    def local_fn(mask_blk, user_sh, item_sh, triples):
        users, items = mask_blk.shape
        cols, own_users = user_sh.shape[1], user_sh.shape[0]
        quarter = items // NQ
        home = triples.shape[0] // NQ
        vm = pltpu.VMEM
        nl = NUM_LAYERS
        scratch = [
            vm((NQ, users, quarter), jnp.int32), vm((NQ, users, quarter), BF16),
            vm((NQ, 1, quarter), F32), vm((NQ, 1, quarter), F32), vm((NQ, 1, quarter), F32),
            vm((NQ, 1, quarter), F32), vm((NQ, 1, quarter), F32),
            vm((users, 128), jnp.int32), vm((1, users), F32), vm((1, users), F32), vm((users, 128), F32),
            vm(triples.shape[::-1], jnp.int32),
            vm((nl + 1, cols, users), BF16), vm((nl, cols, users), F32), vm((nl, cols, users), F32),
            vm((nl + 1, NQ, cols, quarter), BF16), vm((nl, NQ, cols, quarter), F32),
            vm((nl, 2, cols, quarter), F32), vm((nl, cols, quarter), F32), vm((nl, cols, quarter), F32),
            vm((NQ, GL, home), BF16), vm((NQ, GL, home), BF16), vm((GL, home), BF16),
            vm((NQ, 1, home), jnp.int32), vm((NQ, 1, home), jnp.int32), vm((1, home), jnp.int32),
            vm((NQ, cols, home), F32), vm((2, cols, home), F32), vm((2, cols, home), F32),
            vm((cols, home), F32), vm((cols, home), F32),
            vm((NQ, cols, users), BF16), vm((4, 1, home), F32), vm((NQ, 1, home), F32),
            pltpu.SemaphoreType.DMA((NQ + 3,)),
            pltpu.SemaphoreType.DMA((NUM_SEMS,)), pltpu.SemaphoreType.DMA((NUM_SEMS,)),
        ]
        vspec = pl.BlockSpec(memory_space=pltpu.VMEM)
        out_u, out_i, loss = pl.pallas_call(
            kernel,
            out_shape=[
                jax.ShapeDtypeStruct((cols, own_users), BF16),
                jax.ShapeDtypeStruct((cols, quarter), BF16),
                jax.ShapeDtypeStruct((NQ, 1, home), F32)],
            in_specs=[pl.BlockSpec(memory_space=pl.ANY)] * 4,
            out_specs=[vspec, vspec, vspec],
            scratch_shapes=scratch,
            compiler_params=pltpu.CompilerParams(
                collective_id=0, has_side_effects=True, vmem_limit_bytes=60 * 1024 * 1024),
        )(mask_blk, user_sh.T, item_sh.T, triples.T)
        out_u, out_i, loss = pl.pallas_call(
            emit,
            out_shape=[
                jax.ShapeDtypeStruct((cols, own_users), BF16),
                jax.ShapeDtypeStruct((cols, quarter), BF16),
                jax.ShapeDtypeStruct((NQ, 1, home), F32)],
            in_specs=[vspec] * 3, out_specs=[vspec] * 3,
        )(out_u, out_i, loss)
        return out_u.T, out_i.T, loss.reshape(-1)

    return jax.shard_map(
        local_fn, mesh=mesh,
        in_specs=(P("row", "col"), P(("row", "col"), "emb"), P(("col", "row"), "emb"), P()),
        out_specs=(P(("row", "col"), "emb"), P(("col", "row"), "emb"), P()),
        check_vma=False)
```

time: 84.7 us -> 76.6 us (0.904)
  local copies, waits for them, and re-layouts: 4.15 us -> 0 us
  Pallas kernels: 79.7 us -> 75.8 us
    pallas_call x1, Pallas kernels: 79.7 us -> 74.2 us  [local_fn(): pl.pallas_call(kernel, out_shape=[jax.ShapeDtypeStruct((cols, own_users),...]
    unnamed x3 -> x0, local copies, waits for them, and re-layouts: 4.15 us -> none
    pallas_call x0 -> x1, Pallas kernels: none -> 1.57 us  [local_fn(): pl.pallas_call(emit, out_shape=[jax.ShapeDtypeStruct((cols, own_users), B...]
where the time goes in v2:
time: 76.6 us; the launch traced here: 76.5 us
  Pallas kernels  75.8 us (99%)
    pallas_call x1, Pallas kernels, local_fn(): pl.pallas_call(kernel, out_shape=[jax.ShapeDtypeStruct((cols, own_users),...  74.2 us
    pallas_call x1, Pallas kernels, local_fn(): pl.pallas_call(emit, out_shape=[jax.ShapeDtypeStruct((cols, own_users), B...  1.57 us

profile of v2, /device:TPU:0, one launch (start us, length us, event | category | flops | bytes accessed | tf_op | source)
XLA Modules:
  0.0 76.5 jit_solution(8641144398351368308)
XLA Ops:
  0.6 74.2 %shard_map.67 = (bf16[16,128]{1,0:T(8,128)(2,1)}, bf16[16,4096]{1,0:T(8,128)(2,1)}, f32[4,1,1024]{2,1,0:T(1,128)}) custom-call(s32[256,16384]{1,0:T(8,128)} %mask_hbm.1, bf16[16,128]{1,0:T(8,128)(2,1)} %bitcast.8, bf16[16,4096]{1,0:T(8,128)(2,1)} %bitcast.6, s32[3,4096]{1,0:T(4,128)} %bitcast.7), custom_call_target="tpu_custom_call" | custom-call | tf_op jit(solution)/shard_map/pallas_call | solution.py:515
  74.9 1.6 %shard_map.68 = (bf16[16,128]{1,0:T(8,128)(2,1)}, bf16[16,4096]{1,0:T(8,128)(2,1)}, f32[4,1,1024]{2,1,0:T(1,128)}) custom-call(bf16[16,128]{1,0:T(8,128)(2,1)} %get-tuple-element.9.u_in, bf16[16,4096]{1,0:T(8,128)(2,1)} %get-tuple-element.10.i_in, f32[4,1,1024]{2,1,0:T(1,128)} %get-tuple-element.11.l_in), custom_call_target="tpu_custom_call" | custom-call | tf_op jit(solution)/shard_map/pallas_call | solution.py:527

commit v3 on v2

v3 whole, which is shorter than its diff:
```python
import functools

import jax
import jax.numpy as jnp
from jax import lax
from jax.experimental import pallas as pl
from jax.experimental.pallas import tpu as pltpu
from jax.sharding import PartitionSpec as P

NUM_LAYERS = 3
MESH = pl.DeviceIdType.MESH
F32 = jnp.float32
BF16 = jnp.bfloat16

NQ = 4
NM = 2
NS = 4
LB = 256
GL = 256


class Copies:
    def __init__(self, send_sems, recv_sems):
        self.send_sems, self.recv_sems, self.started = send_sems, recv_sems, []

    def send(self, src, dst, device):
        k = len(self.started)
        copy = pltpu.make_async_remote_copy(
            src_ref=src, dst_ref=dst, send_sem=self.send_sems.at[k],
            recv_sem=self.recv_sems.at[k], device_id=device, device_id_type=MESH)
        copy.start()
        self.started.append(copy)
        return copy

    def drain(self):
        for copy in self.started:
            copy.wait_send()


NUM_SEMS = 120


class Phase:
    def __init__(self):
        self.current = None

    def __call__(self, name):
        if self.current is not None:
            self.current.__exit__(None, None, None)
        self.current = None
        if name:
            self.current = jax.named_scope(name)
            self.current.__enter__()


def kernel(mask_hbm, u0_hbm, i0_hbm, trip_hbm, outu_ref, outi_ref, loss_ref,
           maskv, maskb, adj, csum, crd, crx, cch, invi, racc, rsum, rrecv, invu, trip_ref,
           upan, upart, urecv, ipan, ipart, ird, irx, isum,
           ohp, ohn, ohu, hip, hin, hiu, gpart, gsum, grd, grx, gry, eu, zbuf, lossb,
           in_sems, send_sems, recv_sems):
    users = maskv.shape[1]
    quarter = maskv.shape[2]
    own_users = u0_hbm.shape[1]
    sc = quarter // NS
    home = gpart.shape[2]
    hh = home // 2

    z = lax.axis_index("emb")
    y = lax.axis_index("col")
    r = lax.axis_index("row")
    x = r // 2
    c = r % 2
    nz = 4

    def rel(m):
        xx = x if m < 2 else 1 - x
        cc = c if m % 2 == 0 else 1 - c
        return 2 * xx + cc

    dev_d = (z, y, rel(1))
    dev_x = (z, y, rel(2))
    dev_xd = (z, y, rel(3))
    dev_y = (z, 1 - y, r)
    dev_z = [((z + k) % nz, y, r) for k in (1, 2, 3)]

    cp = Copies(send_sems, recv_sems)
    phase = Phase()
    phase("start")

    def load(src, dst, k):
        copy = pltpu.make_async_copy(src, dst, in_sems.at[k])
        copy.start()
        return copy

    y_off = pl.multiple_of(y * own_users, own_users)
    mask_copies = {}
    mh = quarter // NM
    for m in (3, 2, 1, 0):
        for h in range(NM):
            off = pl.multiple_of(rel(m) * quarter + h * mh, mh)
            mask_copies[m, h] = load(
                mask_hbm.at[:, pl.ds(off, mh)], maskv.at[m, :, pl.ds(h * mh, mh)], m * NM + h)
        if m == 3:
            u0_in = load(u0_hbm, upan.at[0, :, pl.ds(y_off, own_users)], NQ * NM)
            i0_in = load(i0_hbm, ipan.at[0, 0], NQ * NM + 1)
            trip_in = load(trip_hbm, trip_ref, NQ * NM + 2)

    barrier = pltpu.get_barrier_semaphore()
    for dev in (dev_d, dev_x, dev_xd, dev_y, *dev_z):
        pl.semaphore_signal(barrier, inc=1, device_id=dev, device_id_type=MESH)

    racc[...] = jnp.zeros_like(racc)

    def sums(m):
        for h in range(NM):
            mask_copies[m, h].wait()

            def body(j, carry):
                off = pl.multiple_of(h * mh + j * LB, LB)
                tile = h * (mh // 128) + j * (LB // 128)
                part = None
                for i in range(users // 16):
                    rows = pl.ds(16 * i, 16)
                    blk = maskv[m, rows, pl.ds(off, LB)]
                    ones = blk.astype(F32).astype(BF16)
                    for g in range(LB // 128):
                        maskb[m, tile + g, rows, :] = ones[:, 128 * g:128 * (g + 1)]
                    two = blk[:8] + blk[8:]
                    part = two if part is None else part + two
                    row = blk[:, :128]
                    for g in range(1, LB // 128):
                        row = row + blk[:, 128 * g:128 * (g + 1)]
                    racc[rows, :] += row
                csum[m, :, pl.ds(off, LB)] = jnp.sum(part.astype(F32), axis=0, keepdims=True)
                return carry
            lax.fori_loop(0, mh // LB, body, 0)

    def one_hot(lanes):
        hit = lax.broadcasted_iota(jnp.int32, (GL, 128), 0) == lanes
        return jnp.where(hit, 1.0, 0.0).astype(BF16)

    def hot_block(oh, t):
        n = LB // 128
        return jnp.concatenate([oh[t * n + i] for i in range(n)], axis=1)

    def one_hots(m):
        base = pl.multiple_of(rel(m) * home, home)
        for row, oh, hi in ((1, ohp, hip), (2, ohn, hin)):
            ids = trip_ref[pl.ds(row, 1), pl.ds(base, home)]
            owned = ids // quarter == y * NQ + r
            hi[m] = (ids % quarter) // GL
            low = jnp.where(owned, ids % GL, -1)
            for t in range(home // 128):
                oh[m, t] = one_hot(low[:, t * 128:(t + 1) * 128])

    def user_one_hots():
        base = pl.multiple_of(r * home, home)
        uids = trip_ref[pl.ds(0, 1), pl.ds(base, home)]
        hiu[...] = uids // users
        low = uids % users
        for t in range(home // 128):
            ohu[t] = one_hot(low[:, t * 128:(t + 1) * 128])

    csum_d, csum_x = {}, {}

    def chip_sums(m):
        csum_d[m].wait_recv()
        cch[m] = csum[m] + crd[m]
        csum_x[m ^ 2] = cp.send(cch.at[m], crx.at[m ^ 2], dev_x)

    def send_sums(m):
        csum_d[m ^ 1] = cp.send(csum.at[m], crd.at[m ^ 1], dev_d)

    phase("sums32")
    sums(3)
    sums(2)
    u0_in.wait()
    i0_in.wait()
    trip_in.wait()
    phase("barrier")
    pl.semaphore_wait(barrier, 7)
    phase("sums10")
    send_sums(3)
    send_sums(2)
    u0_y = cp.send(upan.at[0, :, pl.ds(y_off, own_users)], upan.at[0, :, pl.ds(y_off, own_users)], dev_y)
    i0_d = cp.send(ipan.at[0, 0], ipan.at[0, 1], dev_d)
    sums(1)
    send_sums(1)
    chip_sums(3)
    chip_sums(2)
    sums(0)
    send_sums(0)
    phase("rows")
    rows = jnp.transpose(racc[...].astype(F32), (1, 0))
    rsum[...] = jnp.sum(rows, axis=0, keepdims=True)
    rs_y = cp.send(rsum, rrecv, dev_y)
    chip_sums(1)
    one_hots(3)
    phase("chip0")
    chip_sums(0)
    i0_x = cp.send(ipan.at[0, 0], ipan.at[0, 2], dev_x)
    phase("onehots")
    one_hots(2)
    one_hots(1)
    phase("rs_wait")
    u0_y.wait_recv()
    rs_y.wait_recv()
    inv_row = lax.rsqrt(jnp.maximum(rsum[...] + rrecv[...], 1.0))
    invu[...] = jnp.transpose(jnp.broadcast_to(inv_row, (128, users)), (1, 0))
    phase("cx_wait")
    for m in (3, 2, 1, 0):
        csum_x[m].wait_recv()
        invi[m] = lax.rsqrt(jnp.maximum(cch[m] + crx[m], 1.0))

    def build(m, s):
        for g in range(sc // 128):
            lanes = slice(s * sc + 128 * g, s * sc + 128 * (g + 1))
            scale = (invu[...] * invi[m, :, lanes]).astype(BF16)
            tile = s * (sc // 128) + g
            adj[m, tile] = scale * maskb[m, tile]

    def block(m, s, n, rows):
        first, count = s * (sc // 128), n * (sc // 128)
        return jnp.concatenate([adj[m, first + t, rows, :] for t in range(count)], axis=1)

    def item_piece(k, m, s):
        sl = pl.ds(s * sc, sc)
        ipart[k, m, :, sl] = jnp.dot(upan[k], block(m, s, 1, slice(0, users)), preferred_element_type=F32)

    def user_piece(k, m, s, n, acc=None):
        out = []
        for h in (0, 1):
            part = lax.dot_general(
                ipan[k, m, :, s * sc:(s + n) * sc], block(m, s, n, slice(h * own_users, (h + 1) * own_users)),
                (((1,), (1,)), ((), ())), preferred_element_type=F32)
            out.append(part if acc is None else acc[h] + part)
        return out

    def to_core(k, m, s):
        sl = pl.ds(s * sc, sc)
        return cp.send(ipart.at[k, m, :, sl], ird.at[k, (m ^ 1) // 2, :, sl], dev_d)

    def to_x(k, s, got):
        sl = pl.ds(s * sc, sc)
        got.wait_recv()
        isum[k, :, sl] = ipart[k, 2, :, sl] + ird[k, 1, :, sl]
        return cp.send(isum.at[k, :, sl], irx.at[k, :, sl], dev_x)

    def own_piece(k, s, got_d, got_x):
        sl = pl.ds(s * sc, sc)
        got_d.wait_recv()
        got_x.wait_recv()
        total = (ipart[k, 0, :, sl] + ird[k, 0, :, sl]) + irx[k, :, sl]
        ipan[k + 1, 0, :, sl] = total.astype(BF16)

    def gather_piece(k, s):
        sl = pl.ds(s * sc, sc)
        gx = cp.send(ipan.at[k, 0, :, sl], ipan.at[k, 2, :, sl], dev_x)
        gd = cp.send(ipan.at[k, 0, :, sl], ipan.at[k, 1, :, sl], dev_d)
        return gx, gd

    def forward_piece(k, s, gx):
        sl = pl.ds(s * sc, sc)
        gx.wait_recv()
        return cp.send(ipan.at[k, 2, :, sl], ipan.at[k, 3, :, sl], dev_d)

    def send_user(k, acc):
        for h in (0, 1):
            upart[k, :, h * own_users:(h + 1) * own_users] = acc[h]
        return cp.send(upart.at[k], urecv.at[k], dev_y)

    def take_user(k, got):
        got.wait_recv()
        upan[k + 1] = (upart[k] + urecv[k]).astype(BF16)

    d, xs = [{}, {}, {}], [{}, {}, {}]
    g, f = {}, {}

    def own_gather(k, s):
        own_piece(k, s, d[k][0, s], xs[k][s])
        g[k + 1, s] = gather_piece(k + 1, s)

    def core_send(k, m, s):
        d[k][m ^ 1, s] = to_core(k, m, s)

    def x_send(k, s):
        xs[k][s] = to_x(k, s, d[k][2, s])

    def forward(k, s):
        f[k, s] = forward_piece(k, s, g[k, s][0])

    phase("build32")
    build(3, 0)
    for s in range(NS):
        item_piece(0, 3, s)
        build(2, s)
        core_send(0, 3, s)
        item_piece(0, 2, s)
        if s + 1 < NS:
            build(3, s + 1)
        if s:
            x_send(0, s - 1)
    phase("build10")
    build(1, 0)
    x_send(0, NS - 1)
    for s in range(NS):
        item_piece(0, 1, s)
        build(0, s)
        core_send(0, 1, s)
        item_piece(0, 0, s)
        if s + 1 < NS:
            build(1, s + 1)
    phase("upart0")
    i0_d.wait_recv()
    acc = user_piece(0, 1, 0, NS, user_piece(0, 0, 0, NS))
    i0_x.wait_recv()
    i0_f = cp.send(ipan.at[0, 2], ipan.at[0, 3], dev_d)
    phase("own1_0")
    own_gather(0, 0)
    phase("upart0b")
    acc = user_piece(0, 2, 0, NS, acc)
    i0_f.wait_recv()
    acc = user_piece(0, 3, 0, NS, acc)
    u1 = send_user(0, acc)
    phase("own1_1")
    own_gather(0, 1)
    one_hots(0)
    phase("own1_2")
    own_gather(0, 2)
    user_one_hots()
    phase("own1_3")
    own_gather(0, 3)
    phase("u1_wait")
    take_user(0, u1)
    phase("items2_32")

    def items_32(k):
        item_piece(k, 3, 0)
        item_piece(k, 3, 1)
        item_piece(k, 3, 2)
        core_send(k, 3, 0)
        core_send(k, 3, 1)
        item_piece(k, 3, 3)
        item_piece(k, 2, 0)
        core_send(k, 3, 2)
        core_send(k, 3, 3)
        item_piece(k, 2, 1)
        item_piece(k, 2, 2)
        item_piece(k, 2, 3)

    items_32(1)
    phase("fwd1_0")
    forward(1, 0)
    phase("items2_10")
    item_piece(1, 1, 0)
    item_piece(1, 1, 1)
    x_send(1, 0)
    x_send(1, 1)
    item_piece(1, 1, 2)
    item_piece(1, 1, 3)
    x_send(1, 2)
    x_send(1, 3)
    phase("fwd1_1")
    forward(1, 1)
    item_piece(1, 0, 0)
    for s in range(NS):
        core_send(1, 1, s)
    item_piece(1, 0, 1)
    item_piece(1, 0, 2)
    item_piece(1, 0, 3)
    phase("upart1_0")
    acc = user_piece(1, 0, 0, NS)
    phase("fwd1_2")
    forward(1, 2)
    for s in range(NS):
        g[1, s][1].wait_recv()
    acc = user_piece(1, 1, 0, NS, acc)
    phase("fwd1_3")
    forward(1, 3)
    acc = user_piece(1, 2, 0, NS, acc)
    f[1, 0].wait_recv()
    f[1, 1].wait_recv()
    acc = user_piece(1, 3, 0, 2, acc)
    phase("f1_wait")
    f[1, 2].wait_recv()
    f[1, 3].wait_recv()
    acc = user_piece(1, 3, 2, 2, acc)
    u2 = send_user(1, acc)
    phase("own2_01")
    own_gather(1, 0)
    own_gather(1, 1)
    phase("u2_wait")
    take_user(1, u2)
    phase("items3_32")
    items_32(2)
    phase("items3_10")
    item_piece(2, 1, 0)
    item_piece(2, 1, 1)
    x_send(2, 0)
    x_send(2, 1)
    item_piece(2, 1, 2)
    item_piece(2, 1, 3)
    x_send(2, 2)
    x_send(2, 3)
    item_piece(2, 0, 0)
    for s in range(NS):
        core_send(2, 1, s)
    item_piece(2, 0, 1)
    item_piece(2, 0, 2)
    item_piece(2, 0, 3)
    phase("own2_23")
    own_gather(1, 2)
    own_gather(1, 3)
    phase("upart2_01")
    acc = user_piece(2, 0, 0, NS)
    for s in range(NS):
        g[2, s][1].wait_recv()
    acc = user_piece(2, 1, 0, NS, acc)
    phase("fwd2_01")
    forward(2, 0)
    forward(2, 1)
    acc = user_piece(2, 2, 0, 2, acc)
    f[2, 0].wait_recv()
    f[2, 1].wait_recv()
    acc = user_piece(2, 3, 0, 2, acc)

    def pick(tab, oh, hi, n):
        got = jnp.dot(tab, oh, preferred_element_type=F32)
        rows16 = got.shape[0] // n
        out = jnp.where(hi == 0, got[:rows16], 0.0)
        for g0 in range(1, n):
            out = out + jnp.where(hi == g0, got[g0 * rows16:(g0 + 1) * rows16], 0.0)
        return out

    def final_piece(s):
        own_piece(2, s, d[2][0, s], xs[2][s])
        sl = pl.ds(s * sc, sc)
        tot = ((ipan[0, 0, :, sl].astype(F32) + ipan[1, 0, :, sl].astype(F32))
               + ipan[2, 0, :, sl].astype(F32)) + ipan[3, 0, :, sl].astype(F32)
        outi_ref[:, sl] = (tot * (1.0 / (NUM_LAYERS + 1))).astype(BF16)

    half = [pl.ds(0, hh), pl.ds(hh, hh)]

    def differences(m, h):
        for t in range(h * (hh // LB), (h + 1) * (hh // LB)):
            sl = slice(t * LB, (t + 1) * LB)
            pos = pick(table, hot_block(ohp.at[m], t), hip[m, :, sl], quarter // GL)
            neg = pick(table, hot_block(ohn.at[m], t), hin[m, :, sl], quarter // GL)
            gpart[m, :, sl] = pos - neg

    phase("own3")
    for s in range(NS):
        final_piece(s)
    table = jnp.concatenate(
        [outi_ref[:, g0 * GL:(g0 + 1) * GL] for g0 in range(quarter // GL)], axis=0)
    gd3, gd1, gx, gy = {}, {}, {}, {}
    phase("diff3")
    differences(3, 0)
    gd3[0] = cp.send(gpart.at[3, :, half[0]], grd.at[1, :, half[0]], dev_d)
    differences(3, 1)
    gd3[1] = cp.send(gpart.at[3, :, half[1]], grd.at[1, :, half[1]], dev_d)
    differences(2, 0)
    differences(2, 1)
    phase("gd3_wait")
    for h in (0, 1):
        gd3[h].wait_recv()
        gsum[1, :, half[h]] = gpart[2, :, half[h]] + grd[1, :, half[h]]
        gx[h] = cp.send(gsum.at[1, :, half[h]], grx.at[:, half[h]], dev_x)
    phase("diff1")
    differences(1, 0)
    differences(1, 1)
    for h in (0, 1):
        gd1[h] = cp.send(gpart.at[1, :, half[h]], grd.at[0, :, half[h]], dev_d)
    differences(0, 0)
    differences(0, 1)
    phase("fwd2_23")
    forward(2, 2)
    forward(2, 3)
    acc = user_piece(2, 2, 2, 2, acc)
    phase("f2_wait")
    f[2, 2].wait_recv()
    f[2, 3].wait_recv()
    acc = user_piece(2, 3, 2, 2, acc)
    u3 = send_user(2, acc)
    phase("g_wait")
    for h in (0, 1):
        gd1[h].wait_recv()
        gx[h].wait_recv()
        gsum[0, :, half[h]] = (gpart[0, :, half[h]] + grd[0, :, half[h]]) + grx[:, half[h]]
        gy[h] = cp.send(gsum.at[0, :, half[h]], gry.at[:, half[h]], dev_y)

    phase("u3_wait")
    take_user(2, u3)
    phase("finalu")
    ut = ((upan[0].astype(F32) + upan[1].astype(F32)) + upan[2].astype(F32)) + upan[3].astype(F32)
    eu[0] = (ut * (1.0 / (NUM_LAYERS + 1))).astype(BF16)
    e1 = cp.send(eu.at[0], eu.at[1], dev_d)
    e2 = cp.send(eu.at[0], eu.at[2], dev_x)
    e3 = cp.send(eu.at[0], eu.at[3], dev_xd)
    outu_ref[...] = eu[0, :, pl.ds(y_off, own_users)]

    phase("e_wait")
    e1.wait_recv()
    e2.wait_recv()
    e3.wait_recv()
    phase("picku")
    utab = jnp.concatenate([eu[m] for m in range(NQ)], axis=0)
    blk_id = hiu[...]
    place = jnp.where(blk_id // 2 == x, 0, 2) + jnp.where(blk_id % 2 == c, 0, 1)
    picked = []
    for t in range(home // LB):
        picked.append(pick(utab, hot_block(ohu, t), place[:, t * LB:(t + 1) * LB], NQ))
    phase("gy_wait")
    gy[0].wait_recv()
    gy[1].wait_recv()
    phase("dot")
    for t in range(home // LB):
        sl = slice(t * LB, (t + 1) * LB)
        diff = gsum[0, :, sl] + gry[:, sl]
        zbuf[z, :, sl] = jnp.sum(picked[t] * diff, axis=0, keepdims=True)
    zc = [cp.send(zbuf.at[z], zbuf.at[z], dev) for dev in dev_z]
    phase("z_wait")
    for copy in zc:
        copy.wait_recv()
    phase("loss")
    score = ((zbuf[0] + zbuf[1]) + zbuf[2]) + zbuf[3]
    neg = -score
    lossb[r] = jnp.maximum(neg, 0.0) + jnp.log1p(jnp.exp(-jnp.abs(neg)))
    lc = [cp.send(lossb.at[r], lossb.at[r], dev) for dev in (dev_d, dev_x, dev_xd)]
    phase("loss_wait")
    for copy in lc:
        copy.wait_recv()
    phase("end")
    loss_ref[...] = lossb[...]
    phase("drain")
    cp.drain()
    phase(None)


def emit(u_in, i_in, l_in, u_out, i_out, l_out):
    u_out[...] = u_in[...]
    i_out[...] = i_in[...]
    l_out[...] = l_in[...]


def solution(mesh):
    def local_fn(mask_blk, user_sh, item_sh, triples):
        users, items = mask_blk.shape
        cols, own_users = user_sh.shape[1], user_sh.shape[0]
        quarter = items // NQ
        home = triples.shape[0] // NQ
        vm = pltpu.VMEM
        nl = NUM_LAYERS
        scratch = [
            vm((NQ, users, quarter), jnp.int32), vm((NQ, quarter // 128, users, 128), BF16),
            vm((NQ, quarter // 128, users, 128), BF16),
            vm((NQ, 1, quarter), F32), vm((NQ, 1, quarter), F32), vm((NQ, 1, quarter), F32),
            vm((NQ, 1, quarter), F32), vm((NQ, 1, quarter), F32),
            vm((users, 128), jnp.int32), vm((1, users), F32), vm((1, users), F32), vm((users, 128), F32),
            vm(triples.shape[::-1], jnp.int32),
            vm((nl + 1, cols, users), BF16), vm((nl, cols, users), F32), vm((nl, cols, users), F32),
            vm((nl + 1, NQ, cols, quarter), BF16), vm((nl, NQ, cols, quarter), F32),
            vm((nl, 2, cols, quarter), F32), vm((nl, cols, quarter), F32), vm((nl, cols, quarter), F32),
            vm((NQ, home // 128, GL, 128), BF16), vm((NQ, home // 128, GL, 128), BF16),
            vm((home // 128, GL, 128), BF16),
            vm((NQ, 1, home), jnp.int32), vm((NQ, 1, home), jnp.int32), vm((1, home), jnp.int32),
            vm((NQ, cols, home), F32), vm((2, cols, home), F32), vm((2, cols, home), F32),
            vm((cols, home), F32), vm((cols, home), F32),
            vm((NQ, cols, users), BF16), vm((4, 1, home), F32), vm((NQ, 1, home), F32),
            pltpu.SemaphoreType.DMA((NQ * NM + 3,)),
            pltpu.SemaphoreType.DMA((NUM_SEMS,)), pltpu.SemaphoreType.DMA((NUM_SEMS,)),
        ]
        vspec = pl.BlockSpec(memory_space=pltpu.VMEM)
        out_u, out_i, loss = pl.pallas_call(
            kernel,
            out_shape=[
                jax.ShapeDtypeStruct((cols, own_users), BF16),
                jax.ShapeDtypeStruct((cols, quarter), BF16),
                jax.ShapeDtypeStruct((NQ, 1, home), F32)],
            in_specs=[pl.BlockSpec(memory_space=pl.ANY)] * 4,
            out_specs=[vspec, vspec, vspec],
            scratch_shapes=scratch,
            compiler_params=pltpu.CompilerParams(
                collective_id=0, has_side_effects=True, vmem_limit_bytes=60 * 1024 * 1024),
        )(mask_blk, user_sh.T, item_sh.T, triples.T)
        out_u, out_i, loss = pl.pallas_call(
            emit,
            out_shape=[
                jax.ShapeDtypeStruct((cols, own_users), BF16),
                jax.ShapeDtypeStruct((cols, quarter), BF16),
                jax.ShapeDtypeStruct((NQ, 1, home), F32)],
            in_specs=[vspec] * 3, out_specs=[vspec] * 3,
        )(out_u, out_i, loss)
        return out_u.T, out_i.T, loss.reshape(-1)

    return jax.shard_map(
        local_fn, mesh=mesh,
        in_specs=(P("row", "col"), P(("row", "col"), "emb"), P(("col", "row"), "emb"), P()),
        out_specs=(P(("row", "col"), "emb"), P(("col", "row"), "emb"), P()),
        check_vma=False)
```

time: 76.6 us -> 62.1 us (0.81)
  Pallas kernels: 75.8 us -> 61.3 us
    pallas_call x1, Pallas kernels: 74.2 us -> 59.7 us  [local_fn(): pl.pallas_call(kernel, out_shape=[jax.ShapeDtypeStruct((cols, own_users),...]
where the time goes in v3:
time: 62.1 us; the launch traced here: 61.9 us
  Pallas kernels  61.3 us (99%)
  between operations  0.64 us (1%)
    pallas_call x1, Pallas kernels, local_fn(): pl.pallas_call(kernel, out_shape=[jax.ShapeDtypeStruct((cols, own_users),...  59.7 us
    pallas_call x1, Pallas kernels, local_fn(): pl.pallas_call(emit, out_shape=[jax.ShapeDtypeStruct((cols, own_users), B...  1.57 us

profile of v3, /device:TPU:0, one launch (start us, length us, event | category | flops | bytes accessed | tf_op | source)
XLA Modules:
  0.0 61.9 jit_solution(17209768276711707936)
XLA Ops:
  0.6 59.7 %shard_map.67 = (bf16[16,128]{1,0:T(8,128)(2,1)}, bf16[16,4096]{1,0:T(8,128)(2,1)}, f32[4,1,1024]{2,1,0:T(1,128)}) custom-call(s32[256,16384]{1,0:T(8,128)} %mask_hbm.1, bf16[16,128]{1,0:T(8,128)(2,1)} %bitcast.8, bf16[16,4096]{1,0:T(8,128)(2,1)} %bitcast.6, s32[3,4096]{1,0:T(4,128)} %bitcast.7), custom_call_target="tpu_custom_call" | custom-call | tf_op jit(solution)/shard_map/pallas_call | solution.py:574
  60.4 1.6 %shard_map.68 = (bf16[16,128]{1,0:T(8,128)(2,1)}, bf16[16,4096]{1,0:T(8,128)(2,1)}, f32[4,1,1024]{2,1,0:T(1,128)}) custom-call(bf16[16,128]{1,0:T(8,128)(2,1)} %get-tuple-element.9.u_in, bf16[16,4096]{1,0:T(8,128)(2,1)} %get-tuple-element.10.i_in, f32[4,1,1024]{2,1,0:T(1,128)} %get-tuple-element.11.l_in), custom_call_target="tpu_custom_call" | custom-call | tf_op jit(solution)/shard_map/pallas_call | solution.py:586

commit v4 on v0

v4 whole, which is shorter than its diff:
```python
import functools

import jax
import jax.numpy as jnp
from jax import lax
from jax.experimental import pallas as pl
from jax.experimental.pallas import tpu as pltpu
from jax.sharding import PartitionSpec as P

NUM_LAYERS = 3
MESH = pl.DeviceIdType.MESH
F32 = jnp.float32
BF16 = jnp.bfloat16

NQ = 4
NM = 2
NS = 4
LB = 256
GL = 256
LANES = 128
ROWS = 16


class Copies:
    def __init__(self, send_sems, recv_sems):
        self.send_sems, self.recv_sems, self.started = send_sems, recv_sems, []

    def send(self, src, dst, device):
        k = len(self.started)
        copy = pltpu.make_async_remote_copy(
            src_ref=src, dst_ref=dst, send_sem=self.send_sems.at[k],
            recv_sem=self.recv_sems.at[k], device_id=device, device_id_type=MESH)
        copy.start()
        self.started.append(copy)
        return copy

    def drain(self):
        for copy in self.started:
            copy.wait_send()


VMEM_LIMIT = 60 * 2 ** 20
NUM_SEMS = 86
NUM_LOADS = NQ * NM + NS + 2


class Phase:
    def __init__(self):
        self.current = None

    def __call__(self, name):
        if self.current is not None:
            self.current.__exit__(None, None, None)
        self.current = None
        if name:
            self.current = jax.named_scope(name)
            self.current.__enter__()


def kernel(mask_hbm, u0_hbm, i0_hbm, trip_hbm, outu_ref, outi_ref, loss_ref,
           maskv, maskb, adj, csum, crd, crx, cch, invi, racc, rsum, rrecv, invu, trip_ref,
           upan, upart, urecv, ipan, ipart, ird, irx, isum,
           ohp, ohn, ohu, hip, hin, hiu, gpart, gsum, grd, grx, gry, eu, zbuf,
           in_sems, send_sems, recv_sems):
    users, quarter = maskv.shape[1:]
    own_users = u0_hbm.shape[1]
    sc = ipan.shape[-1]
    home = gpart.shape[-1]
    hh = home // 2
    mh = quarter // NM
    pieces, halves = range(NS), range(2)
    own, core, other, both = range(NQ)
    order = (both, other, core, own)

    z, y, r = lax.axis_index("emb"), lax.axis_index("col"), lax.axis_index("row")
    x, c = r // 2, r % 2
    nz = zbuf.shape[0]

    def rel(m):
        xx = x if m in (own, core) else 1 - x
        cc = c if m in (own, other) else 1 - c
        return 2 * xx + cc

    dev_d, dev_x, dev_xd = [(z, y, rel(m)) for m in (core, other, both)]
    dev_y = (z, 1 - y, r)
    score_devs = [((z + k) % nz, y, rel(m)) for k in range(nz) for m in range(NQ) if k or m]

    cp = Copies(send_sems, recv_sems)
    phase = Phase()
    phase("start")
    loads = []

    def load(src, dst):
        copy = pltpu.make_async_copy(src, dst, in_sems.at[len(loads)])
        copy.start()
        loads.append(copy)
        return copy

    y_off = pl.multiple_of(y * own_users, own_users)
    own_u = pl.ds(y_off, own_users)
    mask_copies, small = {}, []
    for m in order:
        for h in range(NM):
            off = pl.multiple_of(rel(m) * quarter + h * mh, mh)
            mask_copies[m, h] = load(mask_hbm.at[:, pl.ds(off, mh)], maskv.at[m, :, pl.ds(h * mh, mh)])
        if m == both:
            small.append(load(u0_hbm, upan.at[0, :, own_u]))
            small += [load(i0_hbm.at[:, pl.ds(s * sc, sc)], ipan.at[0, own, s]) for s in pieces]
            small.append(load(trip_hbm, trip_ref))

    barrier = pltpu.get_barrier_semaphore()
    for dev in (dev_y, *score_devs):
        pl.semaphore_signal(barrier, inc=1, device_id=dev, device_id_type=MESH)

    racc[...] = jnp.zeros_like(racc)

    def sums(m):
        for h in range(NM):
            mask_copies[m, h].wait()

            def body(j, carry):
                off = pl.multiple_of(h * mh + j * LB, LB)
                tile = h * (mh // LANES) + j * (LB // LANES)
                part = None
                for i in range(users // ROWS):
                    rows = pl.ds(ROWS * i, ROWS)
                    blk = maskv[m, rows, pl.ds(off, LB)]
                    ones = blk.astype(F32).astype(BF16)
                    row = None
                    for g in range(LB // LANES):
                        lanes = slice(LANES * g, LANES * (g + 1))
                        maskb[m, tile + g, rows, :] = ones[:, lanes]
                        row = blk[:, lanes] if row is None else row + blk[:, lanes]
                    racc[rows, :] += row
                    two = blk[:ROWS // 2] + blk[ROWS // 2:]
                    part = two if part is None else part + two
                csum[m, :, pl.ds(off, LB)] = jnp.sum(part.astype(F32), axis=0, keepdims=True)
                return carry
            lax.fori_loop(0, mh // LB, body, 0)

    def one_hot(lanes):
        hit = lax.broadcasted_iota(jnp.int32, (GL, LANES), 0) == lanes
        return jnp.where(hit, 1.0, 0.0).astype(BF16)

    def hot_block(oh, t):
        n = LB // LANES
        return jnp.concatenate([oh[t * n + i] for i in range(n)], axis=1)

    def one_hots(m):
        base = pl.multiple_of(rel(m) * home, home)
        for row, oh, hi in ((1, ohp, hip), (2, ohn, hin)):
            ids = trip_ref[pl.ds(row, 1), pl.ds(base, home)]
            owned = ids // quarter == y * NQ + r
            hi[m] = (ids % quarter) // GL
            low = jnp.where(owned, ids % GL, -1)
            for t in range(home // LANES):
                oh[m, t] = one_hot(low[:, t * LANES:(t + 1) * LANES])

    def user_one_hots():
        base = pl.multiple_of(r * home, home)
        uids = trip_ref[pl.ds(0, 1), pl.ds(base, home)]
        hiu[...] = uids // users
        low = uids % users
        for t in range(home // LANES):
            ohu[t] = one_hot(low[:, t * LANES:(t + 1) * LANES])

    csum_d, csum_x = {}, {}

    def chip_sums(m):
        csum_d[m].wait_recv()
        cch[m] = csum[m] + crd[m]
        csum_x[m ^ other] = cp.send(cch.at[m], crx.at[m ^ other], dev_x)

    def send_sums(m):
        csum_d[m ^ core] = cp.send(csum.at[m], crd.at[m ^ core], dev_d)

    phase("sums32")
    sums(both)
    sums(other)
    for copy in small:
        copy.wait()
    phase("barrier")
    pl.semaphore_wait(barrier, 1 + len(score_devs))
    phase("sums10")
    send_sums(both)
    send_sums(other)
    u0_y = cp.send(upan.at[0, :, own_u], upan.at[0, :, own_u], dev_y)
    i0_d = cp.send(ipan.at[0, own], ipan.at[0, core], dev_d)
    sums(core)
    send_sums(core)
    chip_sums(both)
    chip_sums(other)
    sums(own)
    send_sums(own)
    phase("rows")
    rows = jnp.transpose(racc[...].astype(F32), (1, 0))
    rsum[...] = jnp.sum(rows, axis=0, keepdims=True)
    rs_y = cp.send(rsum, rrecv, dev_y)
    chip_sums(core)
    one_hots(both)
    phase("chip0")
    chip_sums(own)
    i0_x = cp.send(ipan.at[0, own], ipan.at[0, other], dev_x)
    phase("onehots")
    one_hots(other)
    one_hots(core)
    phase("rs_wait")
    u0_y.wait_recv()
    rs_y.wait_recv()
    inv_row = lax.rsqrt(jnp.maximum(rsum[...] + rrecv[...], 1.0))
    invu[...] = jnp.transpose(jnp.broadcast_to(inv_row, (LANES, users)), (1, 0))
    phase("cx_wait")
    for m in order:
        csum_x[m].wait_recv()
        invi[m] = lax.rsqrt(jnp.maximum(cch[m] + crx[m], 1.0))

    tiles = sc // LANES

    def build(m, s):
        for tile in range(s * tiles, (s + 1) * tiles):
            scale = (invu[...] * invi[m, :, tile * LANES:(tile + 1) * LANES]).astype(BF16)
            adj[m, tile] = scale * maskb[m, tile]

    def block(m, s, n, rows):
        return jnp.concatenate([adj[m, t, rows, :] for t in range(s * tiles, (s + n) * tiles)], axis=1)

    def items(k, m, some=pieces):
        for s in some:
            ipart[k, m, s] = jnp.dot(upan[k], block(m, s, 1, slice(0, users)), preferred_element_type=F32)

    def user_part(k, m, acc=None, s=0, n=NS):
        table = jnp.concatenate([ipan[k, m, s + i] for i in range(n)], axis=1)
        out = []
        for h in halves:
            part = lax.dot_general(
                table, block(m, s, n, slice(h * own_users, (h + 1) * own_users)),
                (((1,), (1,)), ((), ())), preferred_element_type=F32)
            out.append(part if acc is None else acc[h] + part)
        return out

    d, xs, g, gd, f = {}, {}, {}, {}, {}

    def core_send(k, s):
        d[k, s] = cp.send(ipart.at[k, both, s], ird.at[k, 1, s], dev_d)

    def core_send_own(k):
        d[k] = cp.send(ipart.at[k, core], ird.at[k, 0], dev_d)

    def x_send(k, s):
        d[k, s].wait_recv()
        isum[k, s] = ipart[k, other, s] + ird[k, 1, s]
        xs[k, s] = cp.send(isum.at[k, s], irx.at[k, s], dev_x)

    def own_piece(k, s):
        if s == 0:
            d[k].wait_recv()
        xs[k, s].wait_recv()
        total = (ipart[k, own, s] + ird[k, 0, s]) + irx[k, s]
        ipan[k + 1, own, s] = total.astype(BF16)

    def own_gather(k, s):
        own_piece(k, s)
        g[k + 1, s] = cp.send(ipan.at[k + 1, own, s], ipan.at[k + 1, other, s], dev_x)
        if s == NS - 1:
            gd[k + 1] = cp.send(ipan.at[k + 1, own], ipan.at[k + 1, core], dev_d)

    def forward(k, s):
        g[k, s].wait_recv()
        f[k, s] = cp.send(ipan.at[k, other, s], ipan.at[k, both, s], dev_d)

    def send_user(k, acc):
        for h in halves:
            upart[k, :, h * own_users:(h + 1) * own_users] = acc[h]
        return cp.send(upart.at[k], urecv.at[k], dev_y)

    def take_user(k, got):
        got.wait_recv()
        upan[k + 1] = (upart[k] + urecv[k]).astype(BF16)

    last = NS - 1
    phase("build32")
    for s in pieces:
        build(both, s)
        items(0, both, [s])
        build(other, s)
        core_send(0, s)
        items(0, other, [s])
        if s > 1:
            x_send(0, s - 2)
    phase("build10")
    for s in pieces:
        build(core, s)
        if s in (1, last):
            x_send(0, NS - 2 + s // 2)
    for s in pieces:
        build(own, s)
    phase("upart0")
    i0_d.wait_recv()
    acc = user_part(0, core, user_part(0, own))
    i0_x.wait_recv()
    i0_f = cp.send(ipan.at[0, other], ipan.at[0, both], dev_d)
    acc = user_part(0, other, acc)
    phase("upart0b")
    i0_f.wait_recv()
    acc = user_part(0, both, acc)
    u1 = send_user(0, acc)
    phase("items1_10")
    items(0, core)
    core_send_own(0)
    items(0, own)
    one_hots(own)
    user_one_hots()
    for s in range(last):
        phase(f"own1_{s}")
        own_gather(0, s)
    phase("u1_wait")
    take_user(0, u1)

    def items_x(k):
        items(k, both)
        items(k, other, [0])
        for s in pieces:
            core_send(k, s)
        items(k, other, range(1, NS))

    phase("items2_32")
    items_x(1)
    phase("own1_last")
    own_gather(0, last)
    phase("x2")
    for s in pieces:
        x_send(1, s)
    phase("items2_10")
    items(1, core)
    core_send_own(1)
    items(1, own)
    phase("fwd1_0")
    forward(1, 0)
    acc = user_part(1, own)
    phase("fwd1_1")
    forward(1, 1)
    gd[1].wait_recv()
    acc = user_part(1, core, acc)
    phase("fwd1_2")
    forward(1, 2)
    acc = user_part(1, other, acc, 0, last)
    phase("fwd1_3")
    forward(1, last)
    acc = user_part(1, other, acc, last, 1)
    for s in range(last):
        f[1, s].wait_recv()
    acc = user_part(1, both, acc, 0, last)
    phase("f1_wait")
    f[1, last].wait_recv()
    acc = user_part(1, both, acc, last, 1)
    u2 = send_user(1, acc)
    phase("own2_01")
    own_gather(1, 0)
    own_gather(1, 1)
    phase("u2_wait")
    take_user(1, u2)
    phase("items3_32")
    items_x(2)
    items(2, core)
    phase("x3")
    for s in pieces:
        x_send(2, s)
    core_send_own(2)
    phase("own2_2")
    own_gather(1, 2)
    items(2, own)
    phase("own2_3")
    own_gather(1, last)
    phase("upart2_01")
    acc = user_part(2, own)
    gd[2].wait_recv()
    acc = user_part(2, core, acc)
    phase("fwd2_01")
    for s in halves:
        forward(2, s)
    acc = user_part(2, other, acc, 0, 2)
    for s in halves:
        f[2, s].wait_recv()
    acc = user_part(2, both, acc, 0, 2)

    def mean4(a, b, e, h):
        tot = ((a.astype(F32) + b.astype(F32)) + e.astype(F32)) + h.astype(F32)
        return (tot * (1.0 / (NUM_LAYERS + 1))).astype(BF16)

    def pick(tab, oh, hi, first):
        got = jnp.dot(tab, oh, preferred_element_type=F32)
        n = got.shape[0] // ROWS
        out = jnp.where(hi == first, got[:ROWS], 0.0)
        for i in range(1, n):
            out = out + jnp.where(hi == first + i, got[i * ROWS:(i + 1) * ROWS], 0.0)
        return out

    def final_piece(s):
        own_piece(2, s)
        outi_ref[:, s * sc:(s + 1) * sc] = mean4(*[ipan[k, own, s] for k in range(NUM_LAYERS + 1)])

    half = [pl.ds(h * hh, hh) for h in halves]

    def differences(m, h, first, n):
        groups = range(first * sc // GL, (first + n) * sc // GL)
        table = jnp.concatenate([outi_ref[:, i * GL:(i + 1) * GL] for i in groups], axis=0)
        for t in range(h * (hh // LB), (h + 1) * (hh // LB)):
            sl = slice(t * LB, (t + 1) * LB)
            pos = pick(table, hot_block(ohp.at[m], t), hip[m, :, sl], groups[0])
            neg = pick(table, hot_block(ohn.at[m], t), hin[m, :, sl], groups[0])
            gpart[m, :, sl] = pos - neg if first == 0 else (gpart[m, :, sl] + pos) - neg

    phase("own3")
    for s in range(last):
        final_piece(s)
    phase("diff_012")
    for m in order:
        for h in halves:
            differences(m, h, 0, last)
    phase("own3_last")
    final_piece(last)
    gd3, gd1, gx, gy = {}, {}, {}, {}
    phase("diff3")
    for h in halves:
        differences(both, h, last, 1)
        gd3[h] = cp.send(gpart.at[both, :, half[h]], grd.at[1, :, half[h]], dev_d)
    for h in halves:
        differences(other, h, last, 1)
    for h in halves:
        differences(core, h, last, 1)
    gd1 = cp.send(gpart.at[core], grd.at[0], dev_d)
    phase("gd3_wait")
    for h in halves:
        gd3[h].wait_recv()
        gsum[1, :, half[h]] = gpart[other, :, half[h]] + grd[1, :, half[h]]
        gx[h] = cp.send(gsum.at[1, :, half[h]], grx.at[:, half[h]], dev_x)
    phase("diff0")
    for h in halves:
        differences(own, h, last, 1)
    phase("fwd2_23")
    for s in (2, last):
        forward(2, s)
    acc = user_part(2, other, acc, 2, NS - 2)
    phase("f2_wait")
    for s in (2, last):
        f[2, s].wait_recv()
    acc = user_part(2, both, acc, 2, NS - 2)
    u3 = send_user(2, acc)
    phase("g_wait")
    gd1.wait_recv()
    for h in halves:
        gx[h].wait_recv()
        gsum[0, :, half[h]] = (gpart[own, :, half[h]] + grd[0, :, half[h]]) + grx[:, half[h]]
        gy[h] = cp.send(gsum.at[0, :, half[h]], gry.at[:, half[h]], dev_y)

    phase("u3_wait")
    take_user(2, u3)
    phase("finalu")
    eu[own] = mean4(*[upan[k] for k in range(NUM_LAYERS + 1)])
    ec = [cp.send(eu.at[own], eu.at[m], dev) for m, dev in ((core, dev_d), (other, dev_x), (both, dev_xd))]
    outu_ref[...] = eu[own, :, own_u]

    phase("e_wait")
    for copy in ec:
        copy.wait_recv()
    phase("picku")
    utab = jnp.concatenate([eu[m] for m in range(NQ)], axis=0)
    place = jnp.where(hiu[...] // 2 == x, own, other) + jnp.where(hiu[...] % 2 == c, own, core)
    picked = [pick(utab, hot_block(ohu, t), place[:, t * LB:(t + 1) * LB], own) for t in range(home // LB)]
    phase("gy_wait")
    for h in halves:
        gy[h].wait_recv()
    phase("dot")
    for t in range(home // LB):
        sl = slice(t * LB, (t + 1) * LB)
        diff = gsum[0, :, sl] + gry[:, sl]
        zbuf[z, r, :, sl] = jnp.sum(picked[t] * diff, axis=0, keepdims=True)
    zc = [cp.send(zbuf.at[z, r], zbuf.at[z, r], dev) for dev in score_devs]
    phase("z_wait")
    for copy in zc:
        copy.wait_recv()
    phase("loss")
    for q in range(NQ):
        neg = -(((zbuf[0, q] + zbuf[1, q]) + zbuf[2, q]) + zbuf[3, q])
        loss_ref[q] = jnp.maximum(neg, 0.0) + jnp.log1p(jnp.exp(-jnp.abs(neg)))
    phase("drain")
    cp.drain()
    phase(None)
    assert len(cp.started) == NUM_SEMS and len(loads) == NUM_LOADS


def solution(mesh):
    def local_fn(mask_blk, user_sh, item_sh, triples):
        users, items = mask_blk.shape
        cols, own_users = user_sh.shape[1], user_sh.shape[0]
        quarter = items // NQ
        home = triples.shape[0] // NQ
        vm, sem = pltpu.VMEM, pltpu.SemaphoreType.DMA
        nl = NUM_LAYERS
        sc = quarter // NS
        tiles = (NQ, quarter // LANES, users, LANES)
        per_item, hots = (NQ, 1, quarter), (NQ, home // LANES, GL, LANES)
        triple_row = (NQ, 1, home)
        scratch = [
            vm((NQ, users, quarter), jnp.int32), vm(tiles, BF16), vm(tiles, BF16),
            *[vm(per_item, F32)] * 5,
            vm((users, LANES), jnp.int32), vm((1, users), F32), vm((1, users), F32), vm((users, LANES), F32),
            vm(triples.shape[::-1], jnp.int32),
            vm((nl + 1, cols, users), BF16), vm((nl, cols, users), F32), vm((nl, cols, users), F32),
            vm((nl + 1, NQ, NS, cols, sc), BF16), vm((nl, NQ, NS, cols, sc), F32),
            vm((nl, 2, NS, cols, sc), F32), vm((nl, NS, cols, sc), F32), vm((nl, NS, cols, sc), F32),
            vm(hots, BF16), vm(hots, BF16), vm(hots[1:], BF16),
            vm(triple_row, jnp.int32), vm(triple_row, jnp.int32), vm(triple_row[1:], jnp.int32),
            vm((NQ, cols, home), F32), vm((2, cols, home), F32), vm((2, cols, home), F32),
            vm((cols, home), F32), vm((cols, home), F32),
            vm((NQ, cols, users), BF16), vm((mesh.shape["emb"], *triple_row), F32),
            sem((NUM_LOADS,)), sem((NUM_SEMS,)), sem((NUM_SEMS,)),
        ]
        vspec = pl.BlockSpec(memory_space=pltpu.VMEM)
        out_u, out_i, loss = pl.pallas_call(
            kernel,
            out_shape=[
                jax.ShapeDtypeStruct((cols, own_users), BF16),
                jax.ShapeDtypeStruct((cols, quarter), BF16),
                jax.ShapeDtypeStruct((NQ, 1, home), F32)],
            in_specs=[pl.BlockSpec(memory_space=pltpu.HBM)] * 4,
            out_specs=[vspec, vspec, vspec],
            scratch_shapes=scratch,
            compiler_params=pltpu.CompilerParams(
                collective_id=0, has_side_effects=True, vmem_limit_bytes=VMEM_LIMIT),
        )(mask_blk, user_sh.T, item_sh.T, triples.T)
        return out_u.T, out_i.T, loss.reshape(-1)

    return jax.shard_map(
        local_fn, mesh=mesh,
        in_specs=(P("row", "col"), P(("row", "col"), "emb"), P(("col", "row"), "emb"), P()),
        out_specs=(P(("row", "col"), "emb"), P(("col", "row"), "emb"), P()),
        check_vma=False)
```

time: 334 us -> 60.4 us (0.18)
  waiting for transfers between devices: 147 us -> 0 us
  blocking collectives: 58.1 us -> 0 us
  Pallas kernels: 0 us -> 55.3 us
  local copies, waits for them, and re-layouts: 47.1 us -> 4.15 us
  other arithmetic: 34.3 us -> 0 us
  matrix products: 32.3 us -> 0 us
  between operations: 14.3 us -> 0.64 us
    reduce_scatter x6 -> x0, waiting for transfers between devices: 73.7 us -> none  [the longest x3 64.5 us: local_fn(): lax.psum_scatter(item_part, 'row', scatter_dimension=0, tiled=True)]
    psum x2 -> x0, waiting for transfers between devices: 72.7 us -> none  [the longest x1 55.9 us: bpr_terms(): fetched = lax.psum(fetched, ('row', 'col'))]
    pallas_call x0 -> x1, Pallas kernels: none -> 55.3 us  [local_fn(): pl.pallas_call(kernel, out_shape=[jax.ShapeDtypeStruct((cols, own_users),...]
    gather x3 -> x0, local copies, waits for them, and re-layouts: 39.2 us -> none  [lookup_rows(): picked = jnp.take(table, jnp.clip(local_ids, 0, own_rows - 1), axis=0)]
    all_gather x6 -> x0, blocking collectives: 34.1 us -> none  [the longest x3 20.9 us: local_fn(): item_panel = lax.all_gather(item_cur, 'row', axis=0, tiled=True)]
    dot_general x6 -> x0, matrix products: 32.3 us -> none  [the longest x3 16.9 us: local_fn(): lax.dot_general(adj_blk, user_panel, (((0,), (0,)), ((), ())), preferred_...]
    psum x2 -> x0, blocking collectives: 24 us -> none  [the longest x1 18.7 us: bpr_terms(): score = lax.psum(jnp.sum(e_user * (e_pos - e_neg), axis=1), 'emb')]
    convert_element_type x6 -> x0, other arithmetic: 11.3 us -> none  [the longest x1 7.11 us: norm_adjacency(): (inv_user[:, None] * mask_blk.astype(jnp.float32) * inv_item[None, :]).as...]
  transfers between devices with their start and end apart: 8 -> 0, of which waited for: 7 -> 0; matrix products, arithmetic and copies ran while one was open for 17% -> 0% of each run, Pallas kernels for 0% -> 0%
where the time goes in v4:
time: 60.4 us; the launch traced here: 60.1 us
  Pallas kernels  55.3 us (92%)
  local copies, waits for them, and re-layouts  4.15 us (7%)
  between operations  0.64 us (1%)
    pallas_call x1, Pallas kernels, local_fn(): pl.pallas_call(kernel, out_shape=[jax.ShapeDtypeStruct((cols, own_users),...  55.3 us
    unnamed x3, local copies, waits for them, and re-layouts  4.15 us

profile of v4, /device:TPU:0, one launch (start us, length us, event | category | flops | bytes accessed | tf_op | source)
XLA Modules:
  0.0 60.1 jit_solution(18382928373626939073)
XLA Ops:
  0.6 55.3 %shard_map.67 = (bf16[16,128]{1,0:T(8,128)(2,1)}, bf16[16,4096]{1,0:T(8,128)(2,1)}, f32[4,1,1024]{2,1,0:T(1,128)}) custom-call(s32[256,16384]{1,0:T(8,128)} %mask_hbm.1, bf16[16,128]{1,0:T(8,128)(2,1)} %bitcast.10, bf16[16,4096]{1,0:T(8,128)(2,1)} %bitcast.6, s32[3,4096]{1,0:T(4,128)} %bitcast.8), custom_call_target="tpu_custom_call" | custom-call | tf_op jit(solution)/shard_map/pallas_call | solution.py:520
  55.9 1.3 %copy.10 = bf16[128,16]{0,1:T(8,128)(2,1)} copy(bf16[128,16]{0,1:T(8,128)(2,1)} %bitcast.11) | data formatting | bytes 8192
  57.2 1.6 %copy.11 = bf16[4096,16]{0,1:T(8,128)(2,1)} copy(bf16[4096,16]{0,1:T(8,128)(2,1)} %bitcast.7) | data formatting | bytes 262144
  58.8 1.3 %copy.12 = f32[4096]{0:T(1024)} copy(f32[4096]{0:T(1024)} %bitcast.9) | data formatting | bytes 32768

commit v5 on v4

--- a/solution.py
+++ b/solution.py
@@ -39,7 +39,7 @@
             copy.wait_send()
 
 
-VMEM_LIMIT = 60 * 2 ** 20
+VMEM_LIMIT = 52 * 2 ** 20
 NUM_SEMS = 86
 NUM_LOADS = NQ * NM + NS + 2
 
@@ -489,6 +489,16 @@
     assert len(cp.started) == NUM_SEMS and len(loads) == NUM_LOADS
 
 
+def emit(*refs):
+    n = len(refs) // 2
+    sems = refs[-1]
+    copies = [pltpu.make_async_copy(src, dst, sems.at[i]) for i, (src, dst) in enumerate(zip(refs[:n], refs[n:]))]
+    for copy in copies:
+        copy.start()
+    for copy in copies:
+        copy.wait()
+
+
 def solution(mesh):
     def local_fn(mask_blk, user_sh, item_sh, triples):
         users, items = mask_blk.shape
@@ -528,7 +538,14 @@
             scratch_shapes=scratch,
             compiler_params=pltpu.CompilerParams(
                 collective_id=0, has_side_effects=True, vmem_limit_bytes=VMEM_LIMIT),
-        )(mask_blk, user_sh.T, item_sh.T, triples.T)
+        )(*[pltpu.with_memory_space_constraint(a, pltpu.HBM) for a in (mask_blk, user_sh.T, item_sh.T, triples.T)])
+        out_u, out_i, loss = pl.pallas_call(
+            emit,
+            out_shape=[jax.ShapeDtypeStruct(a.shape, a.dtype) for a in (out_u, out_i, loss)],
+            in_specs=[vspec] * 3, out_specs=[pl.BlockSpec(memory_space=pltpu.HBM)] * 3,
+            scratch_shapes=[sem((3,))],
+            compiler_params=pltpu.CompilerParams(vmem_limit_bytes=2 ** 20),
+        )(out_u, out_i, loss)
         return out_u.T, out_i.T, loss.reshape(-1)
 
     return jax.shard_map(

time: 60.4 us -> 56.1 us (0.929)
  local copies, waits for them, and re-layouts: 4.15 us -> 0 us
    unnamed x3 -> x0, local copies, waits for them, and re-layouts: 4.15 us -> none
    pallas_call x0 -> x1, Pallas kernels: none -> 0.69 us  [local_fn(): pl.pallas_call(emit, out_shape=[jax.ShapeDtypeStruct(a.shape, a.dtype) fo...]
    pallas_call x1, Pallas kernels: 55.3 us -> 54.7 us  [local_fn(): pl.pallas_call(kernel, out_shape=[jax.ShapeDtypeStruct((cols, own_users),...]
where the time goes in v5:
time: 56.1 us; the launch traced here: 56 us
  Pallas kernels  55.3 us (99%)
  between operations  0.64 us (1%)
    pallas_call x1, Pallas kernels, local_fn(): pl.pallas_call(kernel, out_shape=[jax.ShapeDtypeStruct((cols, own_users),...  54.7 us

profile of v5, /device:TPU:0, one launch (start us, length us, event | category | flops | bytes accessed | tf_op | source)
XLA Modules:
  0.0 56.0 jit_solution(14435358828423966931)
XLA Ops:
  0.6 54.7 %shard_map.67 = (bf16[16,128]{1,0:T(8,128)(2,1)S(1)}, bf16[16,4096]{1,0:T(8,128)(2,1)S(1)}, f32[4,1,1024]{2,1,0:T(1,128)S(1)}) custom-call(s32[256,16384]{1,0:T(8,128)} %mask_hbm.1, bf16[16,128]{1,0:T(8,128)(2,1)} %bitcast.8, bf16[16,4096]{1,0:T(8,128)(2,1)} %bitcast.6, s32[3,4096]{1,0:T(4,128)} %bitcast.7), custom_call_target="tpu_custom_call" | custom-call | tf_op jit(solution)/shard_map/pallas_call | solution.py:530
  55.3 0.7 %shard_map.68 = (bf16[16,128]{1,0:T(8,128)(2,1)}, bf16[16,4096]{1,0:T(8,128)(2,1)}, f32[4,1,1024]{2,1,0:T(1,128)}) custom-call(bf16[16,128]{1,0:T(8,128)(2,1)S(1)} %get-tuple-element.9.refs_0_, bf16[16,4096]{1,0:T(8,128)(2,1)S(1)} %get-tuple-element.10.refs_1_, f32[4,1,1024]{2,1,0:T(1,128)S(1)} %get-tuple-element.11.refs_2_), custom_call_target="tpu_custom_call" | custom-call | tf_op jit(solution)/shard_map/pallas_call | solution.py:542

commit v6 on v5

--- a/solution.py
+++ b/solution.py
@@ -23,24 +23,44 @@
 
 class Copies:
     def __init__(self, send_sems, recv_sems):
-        self.send_sems, self.recv_sems, self.started = send_sems, recv_sems, []
-
-    def send(self, src, dst, device):
-        k = len(self.started)
+        self.send_sems, self.recv_sems = send_sems, recv_sems
+        self.recvs, self.groups, self.single = 0, {}, []
+
+    def recv_sem(self):
+        self.recvs += 1
+        return self.recv_sems.at[self.recvs - 1]
+
+    def send(self, src, dst, device, group=None, whole=None, recv_sem=None):
+        count = len(self.groups) + len(self.single)
+        if group is None:
+            sem = self.send_sems.at[count]
+        else:
+            if group not in self.groups:
+                self.groups[group] = (self.send_sems.at[count], whole)
+            sem = self.groups[group][0]
         copy = pltpu.make_async_remote_copy(
-            src_ref=src, dst_ref=dst, send_sem=self.send_sems.at[k],
-            recv_sem=self.recv_sems.at[k], device_id=device, device_id_type=MESH)
+            src_ref=src, dst_ref=dst, send_sem=sem,
+            recv_sem=self.recv_sem() if recv_sem is None else recv_sem,
+            device_id=device, device_id_type=MESH)
         copy.start()
-        self.started.append(copy)
+        if group is None:
+            self.single.append(copy)
         return copy
 
     def drain(self):
-        for copy in self.started:
+        for copy in self.single:
             copy.wait_send()
+        for sem, whole in self.groups.values():
+            wait_bytes(whole, sem)
+
+
+def wait_bytes(ref, sem):
+    pltpu.make_async_copy(ref, ref, sem).wait()
 
 
 VMEM_LIMIT = 52 * 2 ** 20
-NUM_SEMS = 86
+NUM_SENDS = 35
+NUM_RECVS = 71
 NUM_LOADS = NQ * NM + NS + 2
 
 
@@ -60,7 +80,7 @@
 def kernel(mask_hbm, u0_hbm, i0_hbm, trip_hbm, outu_ref, outi_ref, loss_ref,
            maskv, maskb, adj, csum, crd, crx, cch, invi, racc, rsum, rrecv, invu, trip_ref,
            upan, upart, urecv, ipan, ipart, ird, irx, isum,
-           ohp, ohn, ohu, hip, hin, hiu, gpart, gsum, grd, grx, gry, eu, zbuf,
+           ohp, ohn, ohu, hip, hin, hiu, gpart, gsum, grd, grx, gry, grxy, eu, zbuf,
            in_sems, send_sems, recv_sems):
     users, quarter = maskv.shape[1:]
     own_users = u0_hbm.shape[1]
@@ -74,7 +94,8 @@
 
     z, y, r = lax.axis_index("emb"), lax.axis_index("col"), lax.axis_index("row")
     x, c = r // 2, r % 2
-    nz = zbuf.shape[0]
+    nz = zbuf.shape[0] // NQ
+    slot = z * NQ + r
 
     def rel(m):
         xx = x if m in (own, core) else 1 - x
@@ -82,7 +103,7 @@
         return 2 * xx + cc
 
     dev_d, dev_x, dev_xd = [(z, y, rel(m)) for m in (core, other, both)]
-    dev_y = (z, 1 - y, r)
+    dev_y, dev_xy = (z, 1 - y, r), (z, 1 - y, rel(other))
     score_devs = [((z + k) % nz, y, rel(m)) for k in range(nz) for m in range(NQ) if k or m]
 
     cp = Copies(send_sems, recv_sems)
@@ -109,7 +130,7 @@
             small.append(load(trip_hbm, trip_ref))
 
     barrier = pltpu.get_barrier_semaphore()
-    for dev in (dev_y, *score_devs):
+    for dev in (dev_y, dev_xy, *score_devs):
         pl.semaphore_signal(barrier, inc=1, device_id=dev, device_id_type=MESH)
 
     racc[...] = jnp.zeros_like(racc)
@@ -169,10 +190,10 @@
     def chip_sums(m):
         csum_d[m].wait_recv()
         cch[m] = csum[m] + crd[m]
-        csum_x[m ^ other] = cp.send(cch.at[m], crx.at[m ^ other], dev_x)
+        csum_x[m ^ other] = cp.send(cch.at[m], crx.at[m ^ other], dev_x, "chip", cch)
 
     def send_sums(m):
-        csum_d[m ^ core] = cp.send(csum.at[m], crd.at[m ^ core], dev_d)
+        csum_d[m ^ core] = cp.send(csum.at[m], crd.at[m ^ core], dev_d, "sums", csum)
 
     phase("sums32")
     sums(both)
@@ -180,7 +201,7 @@
     for copy in small:
         copy.wait()
     phase("barrier")
-    pl.semaphore_wait(barrier, 1 + len(score_devs))
+    pl.semaphore_wait(barrier, 2 + len(score_devs))
     phase("sums10")
     send_sums(both)
     send_sums(other)
@@ -241,7 +262,7 @@
     d, xs, g, gd, f = {}, {}, {}, {}, {}
 
     def core_send(k, s):
-        d[k, s] = cp.send(ipart.at[k, both, s], ird.at[k, 1, s], dev_d)
+        d[k, s] = cp.send(ipart.at[k, both, s], ird.at[k, 1, s], dev_d, ("core", k), ipart.at[k, both])
 
     def core_send_own(k):
         d[k] = cp.send(ipart.at[k, core], ird.at[k, 0], dev_d)
@@ -249,7 +270,7 @@
     def x_send(k, s):
         d[k, s].wait_recv()
         isum[k, s] = ipart[k, other, s] + ird[k, 1, s]
-        xs[k, s] = cp.send(isum.at[k, s], irx.at[k, s], dev_x)
+        xs[k, s] = cp.send(isum.at[k, s], irx.at[k, s], dev_x, ("x", k), isum.at[k])
 
     def own_piece(k, s):
         if s == 0:
@@ -260,13 +281,14 @@
 
     def own_gather(k, s):
         own_piece(k, s)
-        g[k + 1, s] = cp.send(ipan.at[k + 1, own, s], ipan.at[k + 1, other, s], dev_x)
+        g[k + 1, s] = cp.send(
+            ipan.at[k + 1, own, s], ipan.at[k + 1, other, s], dev_x, ("gather", k), ipan.at[k + 1, own])
         if s == NS - 1:
             gd[k + 1] = cp.send(ipan.at[k + 1, own], ipan.at[k + 1, core], dev_d)
 
     def forward(k, s):
         g[k, s].wait_recv()
-        f[k, s] = cp.send(ipan.at[k, other, s], ipan.at[k, both, s], dev_d)
+        f[k, s] = cp.send(ipan.at[k, other, s], ipan.at[k, both, s], dev_d, ("forward", k), ipan.at[k, other])
 
     def send_user(k, acc):
         for h in halves:
@@ -363,14 +385,16 @@
     items_x(2)
     items(2, core)
     phase("x3")
-    for s in pieces:
-        x_send(2, s)
+    x_send(2, 0)
     core_send_own(2)
     phase("own2_2")
     own_gather(1, 2)
-    items(2, own)
     phase("own2_3")
     own_gather(1, last)
+    for s in range(1, NS):
+        x_send(2, s)
+    phase("items3_own")
+    items(2, own)
     phase("upart2_01")
     acc = user_part(2, own)
     gd[2].wait_recv()
@@ -382,6 +406,15 @@
     for s in halves:
         f[2, s].wait_recv()
     acc = user_part(2, both, acc, 0, 2)
+    phase("fwd2_23")
+    for s in (2, last):
+        forward(2, s)
+    acc = user_part(2, other, acc, 2, NS - 2)
+    phase("f2_wait")
+    for s in (2, last):
+        f[2, s].wait_recv()
+    acc = user_part(2, both, acc, 2, NS - 2)
+    u3 = send_user(2, acc)
 
     def mean4(a, b, e, h):
         tot = ((a.astype(F32) + b.astype(F32)) + e.astype(F32)) + h.astype(F32)
@@ -417,9 +450,19 @@
     for m in order:
         for h in halves:
             differences(m, h, 0, last)
+    phase("u3_wait")
+    take_user(2, u3)
+    phase("finalu")
+    eu[own] = mean4(*[upan[k] for k in range(NUM_LAYERS + 1)])
+    others = eu.at[pl.ds(core, NQ - 1)]
+    eu_sem = cp.recv_sem()
+    for m, dev in ((core, dev_d), (other, dev_x), (both, dev_xd)):
+        cp.send(eu.at[own], eu.at[m], dev, "eu", others, eu_sem)
+    outu_ref[...] = eu[own, :, own_u]
+
     phase("own3_last")
     final_piece(last)
-    gd3, gd1, gx, gy = {}, {}, {}, {}
+    gd3, gx, gxy = {}, {}, {}
     phase("diff3")
     for h in halves:
         differences(both, h, last, 1)
@@ -434,59 +477,44 @@
         gd3[h].wait_recv()
         gsum[1, :, half[h]] = gpart[other, :, half[h]] + grd[1, :, half[h]]
         gx[h] = cp.send(gsum.at[1, :, half[h]], grx.at[:, half[h]], dev_x)
+        gxy[h] = cp.send(gsum.at[1, :, half[h]], grxy.at[:, half[h]], dev_xy)
     phase("diff0")
     for h in halves:
         differences(own, h, last, 1)
-    phase("fwd2_23")
-    for s in (2, last):
-        forward(2, s)
-    acc = user_part(2, other, acc, 2, NS - 2)
-    phase("f2_wait")
-    for s in (2, last):
-        f[2, s].wait_recv()
-    acc = user_part(2, both, acc, 2, NS - 2)
-    u3 = send_user(2, acc)
-    phase("g_wait")
+    phase("gd1_wait")
     gd1.wait_recv()
-    for h in halves:
-        gx[h].wait_recv()
-        gsum[0, :, half[h]] = (gpart[own, :, half[h]] + grd[0, :, half[h]]) + grx[:, half[h]]
-        gy[h] = cp.send(gsum.at[0, :, half[h]], gry.at[:, half[h]], dev_y)
-
-    phase("u3_wait")
-    take_user(2, u3)
-    phase("finalu")
-    eu[own] = mean4(*[upan[k] for k in range(NUM_LAYERS + 1)])
-    ec = [cp.send(eu.at[own], eu.at[m], dev) for m, dev in ((core, dev_d), (other, dev_x), (both, dev_xd))]
-    outu_ref[...] = eu[own, :, own_u]
-
+    gsum[0] = gpart[own] + grd[0]
+    gy = cp.send(gsum.at[0], gry, dev_y)
     phase("e_wait")
-    for copy in ec:
-        copy.wait_recv()
+    wait_bytes(others, eu_sem)
     phase("picku")
     utab = jnp.concatenate([eu[m] for m in range(NQ)], axis=0)
     place = jnp.where(hiu[...] // 2 == x, own, other) + jnp.where(hiu[...] % 2 == c, own, core)
     picked = [pick(utab, hot_block(ohu, t), place[:, t * LB:(t + 1) * LB], own) for t in range(home // LB)]
     phase("gy_wait")
+    gy.wait_recv()
     for h in halves:
-        gy[h].wait_recv()
+        gx[h].wait_recv()
+        gxy[h].wait_recv()
     phase("dot")
     for t in range(home // LB):
         sl = slice(t * LB, (t + 1) * LB)
-        diff = gsum[0, :, sl] + gry[:, sl]
-        zbuf[z, r, :, sl] = jnp.sum(picked[t] * diff, axis=0, keepdims=True)
-    zc = [cp.send(zbuf.at[z, r], zbuf.at[z, r], dev) for dev in score_devs]
+        diff = (gsum[0, :, sl] + grx[:, sl]) + (gry[:, sl] + grxy[:, sl])
+        zbuf[slot, :, sl] = jnp.sum(picked[t] * diff, axis=0, keepdims=True)
+    rest = zbuf.at[pl.ds(0, len(score_devs))]
+    z_sem = cp.recv_sem()
+    for dev in score_devs:
+        cp.send(zbuf.at[slot], zbuf.at[slot], dev, "score", rest, z_sem)
     phase("z_wait")
-    for copy in zc:
-        copy.wait_recv()
+    wait_bytes(rest, z_sem)
     phase("loss")
     for q in range(NQ):
-        neg = -(((zbuf[0, q] + zbuf[1, q]) + zbuf[2, q]) + zbuf[3, q])
+        neg = -sum(zbuf[k * NQ + q] for k in range(nz))
         loss_ref[q] = jnp.maximum(neg, 0.0) + jnp.log1p(jnp.exp(-jnp.abs(neg)))
     phase("drain")
     cp.drain()
     phase(None)
-    assert len(cp.started) == NUM_SEMS and len(loads) == NUM_LOADS
+    assert (len(cp.groups) + len(cp.single), cp.recvs, len(loads)) == (NUM_SENDS, NUM_RECVS, NUM_LOADS)
 
 
 def emit(*refs):
@@ -522,9 +550,9 @@
             vm(hots, BF16), vm(hots, BF16), vm(hots[1:], BF16),
             vm(triple_row, jnp.int32), vm(triple_row, jnp.int32), vm(triple_row[1:], jnp.int32),
             vm((NQ, cols, home), F32), vm((2, cols, home), F32), vm((2, cols, home), F32),
-            vm((cols, home), F32), vm((cols, home), F32),
-            vm((NQ, cols, users), BF16), vm((mesh.shape["emb"], *triple_row), F32),
-            sem((NUM_LOADS,)), sem((NUM_SEMS,)), sem((NUM_SEMS,)),
+            *[vm((cols, home), F32)] * 3,
+            vm((NQ, cols, users), BF16), vm((mesh.shape["emb"] * NQ, 1, home), F32),
+            sem((NUM_LOADS,)), sem((NUM_SENDS,)), sem((NUM_RECVS,)),
         ]
         vspec = pl.BlockSpec(memory_space=pltpu.VMEM)
         out_u, out_i, loss = pl.pallas_call(

time: 56.1 us -> 55.3 us (0.986)
  Pallas kernels: 55.3 us -> 54.5 us
    pallas_call x1, Pallas kernels: 54.7 us -> 53.8 us  [local_fn(): pl.pallas_call(kernel, out_shape=[jax.ShapeDtypeStruct((cols, own_users),...]
where the time goes in v6:
time: 55.3 us; the launch traced here: 55.1 us
  Pallas kernels  54.5 us (99%)
  between operations  0.64 us (1%)
    pallas_call x1, Pallas kernels, local_fn(): pl.pallas_call(kernel, out_shape=[jax.ShapeDtypeStruct((cols, own_users),...  53.8 us

profile of v6, /device:TPU:0, one launch (start us, length us, event | category | flops | bytes accessed | tf_op | source)
XLA Modules:
  0.0 55.1 jit_solution(12010906252065991877)
XLA Ops:
  0.6 53.8 %shard_map.67 = (bf16[16,128]{1,0:T(8,128)(2,1)S(1)}, bf16[16,4096]{1,0:T(8,128)(2,1)S(1)}, f32[4,1,1024]{2,1,0:T(1,128)S(1)}) custom-call(s32[256,16384]{1,0:T(8,128)} %mask_hbm.1, bf16[16,128]{1,0:T(8,128)(2,1)} %bitcast.8, bf16[16,4096]{1,0:T(8,128)(2,1)} %bitcast.6, s32[3,4096]{1,0:T(4,128)} %bitcast.7), custom_call_target="tpu_custom_call" | custom-call | tf_op jit(solution)/shard_map/pallas_call | solution.py:558
  54.4 0.7 %shard_map.68 = (bf16[16,128]{1,0:T(8,128)(2,1)}, bf16[16,4096]{1,0:T(8,128)(2,1)}, f32[4,1,1024]{2,1,0:T(1,128)}) custom-call(bf16[16,128]{1,0:T(8,128)(2,1)S(1)} %get-tuple-element.9.refs_0_, bf16[16,4096]{1,0:T(8,128)(2,1)S(1)} %get-tuple-element.10.refs_1_, f32[4,1,1024]{2,1,0:T(1,128)S(1)} %get-tuple-element.11.refs_2_), custom_call_target="tpu_custom_call" | custom-call | tf_op jit(solution)/shard_map/pallas_call | solution.py:570

commit v7 on v6

--- a/solution.py
+++ b/solution.py
@@ -316,11 +316,12 @@
             x_send(0, NS - 2 + s // 2)
     for s in pieces:
         build(own, s)
+    phase("i0_x_wait")
+    i0_x.wait_recv()
+    i0_f = cp.send(ipan.at[0, other], ipan.at[0, both], dev_d)
     phase("upart0")
     i0_d.wait_recv()
     acc = user_part(0, core, user_part(0, own))
-    i0_x.wait_recv()
-    i0_f = cp.send(ipan.at[0, other], ipan.at[0, both], dev_d)
     acc = user_part(0, other, acc)
     phase("upart0b")
     i0_f.wait_recv()
@@ -349,13 +350,13 @@
     items_x(1)
     phase("own1_last")
     own_gather(0, last)
-    phase("x2")
-    for s in pieces:
-        x_send(1, s)
     phase("items2_10")
     items(1, core)
     core_send_own(1)
     items(1, own)
+    phase("x2")
+    for s in pieces:
+        x_send(1, s)
     phase("fwd1_0")
     forward(1, 0)
     acc = user_part(1, own)

time: 55.3 us -> 54.1 us (0.978)
  Pallas kernels: 54.5 us -> 53.3 us
    pallas_call x1, Pallas kernels: 53.8 us -> 52.6 us  [local_fn(): pl.pallas_call(kernel, out_shape=[jax.ShapeDtypeStruct((cols, own_users),...]
where the time goes in v7:
time: 54.1 us; the launch traced here: 53.9 us
  Pallas kernels  53.3 us (99%)
  between operations  0.64 us (1%)
    pallas_call x1, Pallas kernels, local_fn(): pl.pallas_call(kernel, out_shape=[jax.ShapeDtypeStruct((cols, own_users),...  52.6 us

profile of v7, /device:TPU:0, one launch (start us, length us, event | category | flops | bytes accessed | tf_op | source)
XLA Modules:
  0.0 53.9 jit_solution(1543186430282985052)
XLA Ops:
  0.6 52.6 %shard_map.67 = (bf16[16,128]{1,0:T(8,128)(2,1)S(1)}, bf16[16,4096]{1,0:T(8,128)(2,1)S(1)}, f32[4,1,1024]{2,1,0:T(1,128)S(1)}) custom-call(s32[256,16384]{1,0:T(8,128)} %mask_hbm.1, bf16[16,128]{1,0:T(8,128)(2,1)} %bitcast.8, bf16[16,4096]{1,0:T(8,128)(2,1)} %bitcast.6, s32[3,4096]{1,0:T(4,128)} %bitcast.7), custom_call_target="tpu_custom_call" | custom-call | tf_op jit(solution)/shard_map/pallas_call | solution.py:559
  53.2 0.7 %shard_map.68 = (bf16[16,128]{1,0:T(8,128)(2,1)}, bf16[16,4096]{1,0:T(8,128)(2,1)}, f32[4,1,1024]{2,1,0:T(1,128)}) custom-call(bf16[16,128]{1,0:T(8,128)(2,1)S(1)} %get-tuple-element.9.refs_0_, bf16[16,4096]{1,0:T(8,128)(2,1)S(1)} %get-tuple-element.10.refs_1_, f32[4,1,1024]{2,1,0:T(1,128)S(1)} %get-tuple-element.11.refs_2_), custom_call_target="tpu_custom_call" | custom-call | tf_op jit(solution)/shard_map/pallas_call | solution.py:571

commit v8 on v7

--- a/solution.py
+++ b/solution.py
@@ -12,6 +12,7 @@
 F32 = jnp.float32
 BF16 = jnp.bfloat16
 
+NY = 2
 NQ = 4
 NM = 2
 NS = 4
@@ -59,8 +60,8 @@
 
 
 VMEM_LIMIT = 52 * 2 ** 20
-NUM_SENDS = 35
-NUM_RECVS = 71
+NUM_SENDS = 33
+NUM_RECVS = 69
 NUM_LOADS = NQ * NM + NS + 2
 
 
@@ -80,13 +81,13 @@
 def kernel(mask_hbm, u0_hbm, i0_hbm, trip_hbm, outu_ref, outi_ref, loss_ref,
            maskv, maskb, adj, csum, crd, crx, cch, invi, racc, rsum, rrecv, invu, trip_ref,
            upan, upart, urecv, ipan, ipart, ird, irx, isum,
-           ohp, ohn, ohu, hip, hin, hiu, gpart, gsum, grd, grx, gry, grxy, eu, zbuf,
+           ohp, ohn, ohu, hip, hin, hiu, gpart, gsum, grd, grx, eu, zbuf,
            in_sems, send_sems, recv_sems):
     users, quarter = maskv.shape[1:]
     own_users = u0_hbm.shape[1]
     sc = ipan.shape[-1]
-    home = gpart.shape[-1]
-    hh = home // 2
+    hh = gpart.shape[-1]
+    home = NY * hh
     mh = quarter // NM
     pieces, halves = range(NS), range(2)
     own, core, other, both = range(NQ)
@@ -94,8 +95,8 @@
 
     z, y, r = lax.axis_index("emb"), lax.axis_index("col"), lax.axis_index("row")
     x, c = r // 2, r % 2
-    nz = zbuf.shape[0] // NQ
-    slot = z * NQ + r
+    nz = zbuf.shape[0] // (NQ * NY)
+    slot = (z * NQ + r) * NY + y
 
     def rel(m):
         xx = x if m in (own, core) else 1 - x
@@ -104,7 +105,7 @@
 
     dev_d, dev_x, dev_xd = [(z, y, rel(m)) for m in (core, other, both)]
     dev_y, dev_xy = (z, 1 - y, r), (z, 1 - y, rel(other))
-    score_devs = [((z + k) % nz, y, rel(m)) for k in range(nz) for m in range(NQ) if k or m]
+    score_devs = [((z + k) % nz, yy, rel(m)) for k in range(nz) for yy in (y, 1 - y) for m in range(NQ)][1:]
 
     cp = Copies(send_sems, recv_sems)
     phase = Phase()
@@ -130,7 +131,7 @@
             small.append(load(trip_hbm, trip_ref))
 
     barrier = pltpu.get_barrier_semaphore()
-    for dev in (dev_y, dev_xy, *score_devs):
+    for dev in score_devs:
         pl.semaphore_signal(barrier, inc=1, device_id=dev, device_id_type=MESH)
 
     racc[...] = jnp.zeros_like(racc)
@@ -178,11 +179,11 @@
                 oh[m, t] = one_hot(low[:, t * LANES:(t + 1) * LANES])
 
     def user_one_hots():
-        base = pl.multiple_of(r * home, home)
-        uids = trip_ref[pl.ds(0, 1), pl.ds(base, home)]
+        base = pl.multiple_of((r * NY + y) * hh, hh)
+        uids = trip_ref[pl.ds(0, 1), pl.ds(base, hh)]
         hiu[...] = uids // users
         low = uids % users
-        for t in range(home // LANES):
+        for t in range(hh // LANES):
             ohu[t] = one_hot(low[:, t * LANES:(t + 1) * LANES])
 
     csum_d, csum_x = {}, {}
@@ -201,7 +202,7 @@
     for copy in small:
         copy.wait()
     phase("barrier")
-    pl.semaphore_wait(barrier, 2 + len(score_devs))
+    pl.semaphore_wait(barrier, len(score_devs))
     phase("sums10")
     send_sums(both)
     send_sums(other)
@@ -433,8 +434,6 @@
         own_piece(2, s)
         outi_ref[:, s * sc:(s + 1) * sc] = mean4(*[ipan[k, own, s] for k in range(NUM_LAYERS + 1)])
 
-    half = [pl.ds(h * hh, hh) for h in halves]
-
     def differences(m, h, first, n):
         groups = range(first * sc // GL, (first + n) * sc // GL)
         table = jnp.concatenate([outi_ref[:, i * GL:(i + 1) * GL] for i in groups], axis=0)
@@ -442,7 +441,8 @@
             sl = slice(t * LB, (t + 1) * LB)
             pos = pick(table, hot_block(ohp.at[m], t), hip[m, :, sl], groups[0])
             neg = pick(table, hot_block(ohn.at[m], t), hin[m, :, sl], groups[0])
-            gpart[m, :, sl] = pos - neg if first == 0 else (gpart[m, :, sl] + pos) - neg
+            out = slice(t * LB - h * hh, (t + 1) * LB - h * hh)
+            gpart[m, h, :, out] = pos - neg if first == 0 else (gpart[m, h, :, out] + pos) - neg
 
     phase("own3")
     for s in range(last):
@@ -463,11 +463,11 @@
 
     phase("own3_last")
     final_piece(last)
-    gd3, gx, gxy = {}, {}, {}
+    gd3 = {}
     phase("diff3")
     for h in halves:
         differences(both, h, last, 1)
-        gd3[h] = cp.send(gpart.at[both, :, half[h]], grd.at[1, :, half[h]], dev_d)
+        gd3[h] = cp.send(gpart.at[both, h], grd.at[1, h], dev_d)
     for h in halves:
         differences(other, h, last, 1)
     for h in halves:
@@ -476,31 +476,32 @@
     phase("gd3_wait")
     for h in halves:
         gd3[h].wait_recv()
-        gsum[1, :, half[h]] = gpart[other, :, half[h]] + grd[1, :, half[h]]
-        gx[h] = cp.send(gsum.at[1, :, half[h]], grx.at[:, half[h]], dev_x)
-        gxy[h] = cp.send(gsum.at[1, :, half[h]], grxy.at[:, half[h]], dev_xy)
+
+    def home_send(i, m, h, dev):
+        gsum[i] = gpart[m, h] + grd[m // 2, h]
+        return cp.send(gsum.at[i], grx.at[i], dev)
+
+    gx = [home_send(0, other, 1 - y, dev_xy), home_send(1, other, y, dev_x)]
     phase("diff0")
     for h in halves:
         differences(own, h, last, 1)
     phase("gd1_wait")
     gd1.wait_recv()
-    gsum[0] = gpart[own] + grd[0]
-    gy = cp.send(gsum.at[0], gry, dev_y)
+    gx.append(home_send(2, own, 1 - y, dev_y))
     phase("e_wait")
     wait_bytes(others, eu_sem)
     phase("picku")
     utab = jnp.concatenate([eu[m] for m in range(NQ)], axis=0)
     place = jnp.where(hiu[...] // 2 == x, own, other) + jnp.where(hiu[...] % 2 == c, own, core)
-    picked = [pick(utab, hot_block(ohu, t), place[:, t * LB:(t + 1) * LB], own) for t in range(home // LB)]
+    picked = [pick(utab, hot_block(ohu, t), place[:, t * LB:(t + 1) * LB], own) for t in range(hh // LB)]
     phase("gy_wait")
-    gy.wait_recv()
-    for h in halves:
-        gx[h].wait_recv()
-        gxy[h].wait_recv()
+    for copy in gx:
+        copy.wait_recv()
     phase("dot")
-    for t in range(home // LB):
+    for t in range(hh // LB):
         sl = slice(t * LB, (t + 1) * LB)
-        diff = (gsum[0, :, sl] + grx[:, sl]) + (gry[:, sl] + grxy[:, sl])
+        mine = gpart[own, y, :, sl] + grd[0, y, :, sl]
+        diff = (mine + grx[1, :, sl]) + (grx[2, :, sl] + grx[0, :, sl])
         zbuf[slot, :, sl] = jnp.sum(picked[t] * diff, axis=0, keepdims=True)
     rest = zbuf.at[pl.ds(0, len(score_devs))]
     z_sem = cp.recv_sem()
@@ -509,8 +510,8 @@
     phase("z_wait")
     wait_bytes(rest, z_sem)
     phase("loss")
-    for q in range(NQ):
-        neg = -sum(zbuf[k * NQ + q] for k in range(nz))
+    for q in range(NQ * NY):
+        neg = -sum(zbuf[k * NQ * NY + q] for k in range(nz))
         loss_ref[q] = jnp.maximum(neg, 0.0) + jnp.log1p(jnp.exp(-jnp.abs(neg)))
     phase("drain")
     cp.drain()
@@ -534,6 +535,7 @@
         cols, own_users = user_sh.shape[1], user_sh.shape[0]
         quarter = items // NQ
         home = triples.shape[0] // NQ
+        hh = home // NY
         vm, sem = pltpu.VMEM, pltpu.SemaphoreType.DMA
         nl = NUM_LAYERS
         sc = quarter // NS
@@ -548,11 +550,10 @@
             vm((nl + 1, cols, users), BF16), vm((nl, cols, users), F32), vm((nl, cols, users), F32),
             vm((nl + 1, NQ, NS, cols, sc), BF16), vm((nl, NQ, NS, cols, sc), F32),
             vm((nl, 2, NS, cols, sc), F32), vm((nl, NS, cols, sc), F32), vm((nl, NS, cols, sc), F32),
-            vm(hots, BF16), vm(hots, BF16), vm(hots[1:], BF16),
-            vm(triple_row, jnp.int32), vm(triple_row, jnp.int32), vm(triple_row[1:], jnp.int32),
-            vm((NQ, cols, home), F32), vm((2, cols, home), F32), vm((2, cols, home), F32),
-            *[vm((cols, home), F32)] * 3,
-            vm((NQ, cols, users), BF16), vm((mesh.shape["emb"] * NQ, 1, home), F32),
+            vm(hots, BF16), vm(hots, BF16), vm((hh // LANES, GL, LANES), BF16),
+            vm(triple_row, jnp.int32), vm(triple_row, jnp.int32), vm((1, hh), jnp.int32),
+            vm((NQ, NY, cols, hh), F32), vm((3, cols, hh), F32), vm((2, NY, cols, hh), F32), vm((3, cols, hh), F32),
+            vm((NQ, cols, users), BF16), vm((mesh.size, 1, hh), F32),
             sem((NUM_LOADS,)), sem((NUM_SENDS,)), sem((NUM_RECVS,)),
         ]
         vspec = pl.BlockSpec(memory_space=pltpu.VMEM)
@@ -561,7 +562,7 @@
             out_shape=[
                 jax.ShapeDtypeStruct((cols, own_users), BF16),
                 jax.ShapeDtypeStruct((cols, quarter), BF16),
-                jax.ShapeDtypeStruct((NQ, 1, home), F32)],
+                jax.ShapeDtypeStruct((NQ * NY, 1, hh), F32)],
             in_specs=[pl.BlockSpec(memory_space=pltpu.HBM)] * 4,
             out_specs=[vspec, vspec, vspec],
             scratch_shapes=scratch,

time: 54.1 us -> 53.4 us (0.987)
  Pallas kernels: 53.3 us -> 52.6 us
    pallas_call x1, Pallas kernels: 52.6 us -> 51.9 us  [local_fn(): pl.pallas_call(kernel, out_shape=[jax.ShapeDtypeStruct((cols, own_users),...]
where the time goes in v8:
time: 53.4 us; the launch traced here: 53.3 us
  Pallas kernels  52.6 us (99%)
  between operations  0.64 us (1%)
    pallas_call x1, Pallas kernels, local_fn(): pl.pallas_call(kernel, out_shape=[jax.ShapeDtypeStruct((cols, own_users),...  51.9 us

profile of v8, /device:TPU:0, one launch (start us, length us, event | category | flops | bytes accessed | tf_op | source)
XLA Modules:
  0.0 53.3 jit_solution(11781640787854040252)
XLA Ops:
  0.6 51.9 %shard_map.67 = (bf16[16,128]{1,0:T(8,128)(2,1)S(1)}, bf16[16,4096]{1,0:T(8,128)(2,1)S(1)}, f32[8,1,512]{2,1,0:T(1,128)S(1)}) custom-call(s32[256,16384]{1,0:T(8,128)} %mask_hbm.1, bf16[16,128]{1,0:T(8,128)(2,1)} %bitcast.8, bf16[16,4096]{1,0:T(8,128)(2,1)} %bitcast.6, s32[3,4096]{1,0:T(4,128)} %bitcast.7), custom_call_target="tpu_custom_call" | custom-call | tf_op jit(solution)/shard_map/pallas_call | solution.py:560
  52.6 0.7 %shard_map.68 = (bf16[16,128]{1,0:T(8,128)(2,1)}, bf16[16,4096]{1,0:T(8,128)(2,1)}, f32[8,1,512]{2,1,0:T(1,128)}) custom-call(bf16[16,128]{1,0:T(8,128)(2,1)S(1)} %get-tuple-element.9.refs_0_, bf16[16,4096]{1,0:T(8,128)(2,1)S(1)} %get-tuple-element.10.refs_1_, f32[8,1,512]{2,1,0:T(1,128)S(1)} %get-tuple-element.11.refs_2_), custom_call_target="tpu_custom_call" | custom-call | tf_op jit(solution)/shard_map/pallas_call | solution.py:572

commit v9 on v8

--- a/solution.py
+++ b/solution.py
@@ -60,8 +60,8 @@
 
 
 VMEM_LIMIT = 52 * 2 ** 20
-NUM_SENDS = 33
-NUM_RECVS = 69
+NUM_SENDS = 31
+NUM_RECVS = 64
 NUM_LOADS = NQ * NM + NS + 2
 
 
@@ -105,7 +105,8 @@
 
     dev_d, dev_x, dev_xd = [(z, y, rel(m)) for m in (core, other, both)]
     dev_y, dev_xy = (z, 1 - y, r), (z, 1 - y, rel(other))
-    score_devs = [((z + k) % nz, yy, rel(m)) for k in range(nz) for yy in (y, 1 - y) for m in range(NQ)][1:]
+    flip = [(1 - z // 2, 1 - z % 2), (1 - z // 2, z % 2), (z // 2, 1 - z % 2), (z // 2, z % 2)]
+    score_devs = [(2 * a + b, yy, rel(m)) for a, b in flip for yy in (1 - y, y) for m in order][:-1]
 
     cp = Copies(send_sems, recv_sems)
     phase = Phase()
@@ -186,12 +187,12 @@
         for t in range(hh // LANES):
             ohu[t] = one_hot(low[:, t * LANES:(t + 1) * LANES])
 
-    csum_d, csum_x = {}, {}
+    csum_d, csum_x = {}, cp.recv_sem()
 
     def chip_sums(m):
         csum_d[m].wait_recv()
         cch[m] = csum[m] + crd[m]
-        csum_x[m ^ other] = cp.send(cch.at[m], crx.at[m ^ other], dev_x, "chip", cch)
+        cp.send(cch.at[m], crx.at[m ^ other], dev_x, "chip", cch, csum_x)
 
     def send_sums(m):
         csum_d[m ^ core] = cp.send(csum.at[m], crd.at[m ^ core], dev_d, "sums", csum)
@@ -232,8 +233,8 @@
     inv_row = lax.rsqrt(jnp.maximum(rsum[...] + rrecv[...], 1.0))
     invu[...] = jnp.transpose(jnp.broadcast_to(inv_row, (LANES, users)), (1, 0))
     phase("cx_wait")
+    wait_bytes(crx, csum_x)
     for m in order:
-        csum_x[m].wait_recv()
         invi[m] = lax.rsqrt(jnp.maximum(cch[m] + crx[m], 1.0))
 
     tiles = sc // LANES
@@ -340,11 +341,13 @@
     phase("u1_wait")
     take_user(0, u1)
 
-    def items_x(k):
+    def items_x(k, between=None):
         items(k, both)
         items(k, other, [0])
         for s in pieces:
             core_send(k, s)
+        if between is not None:
+            between()
         items(k, other, range(1, NS))
 
     phase("items2_32")
@@ -384,13 +387,11 @@
     phase("u2_wait")
     take_user(1, u2)
     phase("items3_32")
-    items_x(2)
+    items_x(2, lambda: own_gather(1, 2))
     items(2, core)
     phase("x3")
     x_send(2, 0)
     core_send_own(2)
-    phase("own2_2")
-    own_gather(1, 2)
     phase("own2_3")
     own_gather(1, last)
     for s in range(1, NS):
@@ -477,17 +478,20 @@
     for h in halves:
         gd3[h].wait_recv()
 
+    g_sem = cp.recv_sem()
+
     def home_send(i, m, h, dev):
         gsum[i] = gpart[m, h] + grd[m // 2, h]
-        return cp.send(gsum.at[i], grx.at[i], dev)
-
-    gx = [home_send(0, other, 1 - y, dev_xy), home_send(1, other, y, dev_x)]
+        cp.send(gsum.at[i], grx.at[i], dev, "home", gsum, g_sem)
+
+    home_send(0, other, 1 - y, dev_xy)
+    home_send(1, other, y, dev_x)
     phase("diff0")
     for h in halves:
         differences(own, h, last, 1)
     phase("gd1_wait")
     gd1.wait_recv()
-    gx.append(home_send(2, own, 1 - y, dev_y))
+    home_send(2, own, 1 - y, dev_y)
     phase("e_wait")
     wait_bytes(others, eu_sem)
     phase("picku")
@@ -495,8 +499,7 @@
     place = jnp.where(hiu[...] // 2 == x, own, other) + jnp.where(hiu[...] % 2 == c, own, core)
     picked = [pick(utab, hot_block(ohu, t), place[:, t * LB:(t + 1) * LB], own) for t in range(hh // LB)]
     phase("gy_wait")
-    for copy in gx:
-        copy.wait_recv()
+    wait_bytes(grx, g_sem)
     phase("dot")
     for t in range(hh // LB):
         sl = slice(t * LB, (t + 1) * LB)

time: 53.4 us -> 52.7 us (0.987)
  Pallas kernels: 52.6 us -> 52 us
    pallas_call x1, Pallas kernels: 51.9 us -> 51.3 us  [local_fn(): pl.pallas_call(kernel, out_shape=[jax.ShapeDtypeStruct((cols, own_users),...]
where the time goes in v9:
time: 52.7 us; the launch traced here: 52.6 us
  Pallas kernels  52 us (99%)
  between operations  0.64 us (1%)
    pallas_call x1, Pallas kernels, local_fn(): pl.pallas_call(kernel, out_shape=[jax.ShapeDtypeStruct((cols, own_users),...  51.3 us

profile of v9, /device:TPU:0, one launch (start us, length us, event | category | flops | bytes accessed | tf_op | source)
XLA Modules:
  0.0 52.6 jit_solution(7213591639318055725)
XLA Ops:
  0.6 51.3 %shard_map.67 = (bf16[16,128]{1,0:T(8,128)(2,1)S(1)}, bf16[16,4096]{1,0:T(8,128)(2,1)S(1)}, f32[8,1,512]{2,1,0:T(1,128)S(1)}) custom-call(s32[256,16384]{1,0:T(8,128)} %mask_hbm.1, bf16[16,128]{1,0:T(8,128)(2,1)} %bitcast.8, bf16[16,4096]{1,0:T(8,128)(2,1)} %bitcast.6, s32[3,4096]{1,0:T(4,128)} %bitcast.7), custom_call_target="tpu_custom_call" | custom-call | tf_op jit(solution)/shard_map/pallas_call | solution.py:563
  51.9 0.7 %shard_map.68 = (bf16[16,128]{1,0:T(8,128)(2,1)}, bf16[16,4096]{1,0:T(8,128)(2,1)}, f32[8,1,512]{2,1,0:T(1,128)}) custom-call(bf16[16,128]{1,0:T(8,128)(2,1)S(1)} %get-tuple-element.9.refs_0_, bf16[16,4096]{1,0:T(8,128)(2,1)S(1)} %get-tuple-element.10.refs_1_, f32[8,1,512]{2,1,0:T(1,128)S(1)} %get-tuple-element.11.refs_2_), custom_call_target="tpu_custom_call" | custom-call | tf_op jit(solution)/shard_map/pallas_call | solution.py:575

commit v10 on v9

--- a/solution.py
+++ b/solution.py
@@ -14,7 +14,7 @@
 
 NY = 2
 NQ = 4
-NM = 2
+NM = 4
 NS = 4
 LB = 256
 GL = 256
@@ -61,8 +61,8 @@
 
 VMEM_LIMIT = 52 * 2 ** 20
 NUM_SENDS = 31
-NUM_RECVS = 64
-NUM_LOADS = NQ * NM + NS + 2
+NUM_RECVS = 57
+NUM_LOADS = NQ * NM + 3
 
 
 class Phase:
@@ -113,10 +113,12 @@
     phase("start")
     loads = []
 
-    def load(src, dst):
-        copy = pltpu.make_async_copy(src, dst, in_sems.at[len(loads)])
+    def load(src, dst, sem=None):
+        if sem is None:
+            loads.append(in_sems.at[len(loads)])
+            sem = loads[-1]
+        copy = pltpu.make_async_copy(src, dst, sem)
         copy.start()
-        loads.append(copy)
         return copy
 
     y_off = pl.multiple_of(y * own_users, own_users)
@@ -128,7 +130,10 @@
             mask_copies[m, h] = load(mask_hbm.at[:, pl.ds(off, mh)], maskv.at[m, :, pl.ds(h * mh, mh)])
         if m == both:
             small.append(load(u0_hbm, upan.at[0, :, own_u]))
-            small += [load(i0_hbm.at[:, pl.ds(s * sc, sc)], ipan.at[0, own, s]) for s in pieces]
+            loads.append(in_sems.at[len(loads)])
+            i0_sem = loads[-1]
+            for s in pieces:
+                load(i0_hbm.at[:, pl.ds(s * sc, sc)], ipan.at[0, own, s], i0_sem)
             small.append(load(trip_hbm, trip_ref))
 
     barrier = pltpu.get_barrier_semaphore()
@@ -202,6 +207,7 @@
     sums(other)
     for copy in small:
         copy.wait()
+    wait_bytes(ipan.at[0, own], i0_sem)
     phase("barrier")
     pl.semaphore_wait(barrier, len(score_devs))
     phase("sums10")
@@ -262,15 +268,25 @@
         return out
 
     d, xs, g, gd, f = {}, {}, {}, {}, {}
+    shared, last = {}, NS - 1
+
+    def share(*name):
+        if name not in shared:
+            shared[name] = cp.recv_sem()
+        return shared[name]
 
     def core_send(k, s):
-        d[k, s] = cp.send(ipart.at[k, both, s], ird.at[k, 1, s], dev_d, ("core", k), ipart.at[k, both])
+        d[k, s] = cp.send(ipart.at[k, both, s], ird.at[k, 1, s], dev_d, ("core", k), ipart.at[k, both],
+            share("core", k) if k == 1 else None)
 
     def core_send_own(k):
         d[k] = cp.send(ipart.at[k, core], ird.at[k, 0], dev_d)
 
     def x_send(k, s):
-        d[k, s].wait_recv()
+        if k != 1:
+            d[k, s].wait_recv()
+        elif s == 0:
+            wait_bytes(ird.at[k, 1], share("core", k))
         isum[k, s] = ipart[k, other, s] + ird[k, 1, s]
         xs[k, s] = cp.send(isum.at[k, s], irx.at[k, s], dev_x, ("x", k), isum.at[k])
 
@@ -288,9 +304,16 @@
         if s == NS - 1:
             gd[k + 1] = cp.send(ipan.at[k + 1, own], ipan.at[k + 1, core], dev_d)
 
+    batches = {1: (range(last), range(last, NS)), 2: (halves, range(2, NS))}
+
+    def take_forwarded(k, i):
+        batch = batches[k][i]
+        wait_bytes(ipan.at[k, both, pl.ds(batch.start, len(batch))], share("forward", k, i == 0))
+
     def forward(k, s):
         g[k, s].wait_recv()
-        f[k, s] = cp.send(ipan.at[k, other, s], ipan.at[k, both, s], dev_d, ("forward", k), ipan.at[k, other])
+        f[k, s] = cp.send(ipan.at[k, other, s], ipan.at[k, both, s], dev_d, ("forward", k), ipan.at[k, other],
+            share("forward", k, s in batches[k][0]))
 
     def send_user(k, acc):
         for h in halves:
@@ -301,15 +324,18 @@
         got.wait_recv()
         upan[k + 1] = (upart[k] + urecv[k]).astype(BF16)
 
-    last = NS - 1
     phase("build32")
-    for s in pieces:
-        build(both, s)
-        items(0, both, [s])
-        build(other, s)
-        core_send(0, s)
-        items(0, other, [s])
-        if s > 1:
+    for s in range(NS + 1):
+        if s < NS:
+            build(both, s)
+            items(0, both, [s])
+        if s:
+            build(other, s - 1)
+        if s < NS:
+            core_send(0, s)
+        if s:
+            items(0, other, [s - 1])
+        if s in range(2, NS):
             x_send(0, s - 2)
     phase("build10")
     for s in pieces:
@@ -333,9 +359,10 @@
     items(0, core)
     core_send_own(0)
     items(0, own)
-    one_hots(own)
-    user_one_hots()
     for s in range(last):
+        if s == last - 1:
+            one_hots(own)
+            user_one_hots()
         phase(f"own1_{s}")
         own_gather(0, s)
     phase("u1_wait")
@@ -374,11 +401,10 @@
     phase("fwd1_3")
     forward(1, last)
     acc = user_part(1, other, acc, last, 1)
-    for s in range(last):
-        f[1, s].wait_recv()
+    take_forwarded(1, 0)
     acc = user_part(1, both, acc, 0, last)
     phase("f1_wait")
-    f[1, last].wait_recv()
+    take_forwarded(1, 1)
     acc = user_part(1, both, acc, last, 1)
     u2 = send_user(1, acc)
     phase("own2_01")
@@ -406,16 +432,14 @@
     for s in halves:
         forward(2, s)
     acc = user_part(2, other, acc, 0, 2)
-    for s in halves:
-        f[2, s].wait_recv()
+    take_forwarded(2, 0)
     acc = user_part(2, both, acc, 0, 2)
     phase("fwd2_23")
     for s in (2, last):
         forward(2, s)
     acc = user_part(2, other, acc, 2, NS - 2)
     phase("f2_wait")
-    for s in (2, last):
-        f[2, s].wait_recv()
+    take_forwarded(2, 1)
     acc = user_part(2, both, acc, 2, NS - 2)
     u3 = send_user(2, acc)
 

time: 52.7 us -> 52.6 us (level)
  no operation moved by 1% of the time
where the time goes in v10:
time: 52.6 us; the launch traced here: 52.4 us
  Pallas kernels  51.8 us (98%)
  between operations  0.64 us (1%)
    pallas_call x1, Pallas kernels, local_fn(): pl.pallas_call(kernel, out_shape=[jax.ShapeDtypeStruct((cols, own_users),...  51.1 us

profile of v10, /device:TPU:0, one launch (start us, length us, event | category | flops | bytes accessed | tf_op | source)
XLA Modules:
  0.0 52.4 jit_solution(17832039560126179161)
XLA Ops:
  0.6 51.1 %shard_map.67 = (bf16[16,128]{1,0:T(8,128)(2,1)S(1)}, bf16[16,4096]{1,0:T(8,128)(2,1)S(1)}, f32[8,1,512]{2,1,0:T(1,128)S(1)}) custom-call(s32[256,16384]{1,0:T(8,128)} %mask_hbm.1, bf16[16,128]{1,0:T(8,128)(2,1)} %bitcast.8, bf16[16,4096]{1,0:T(8,128)(2,1)} %bitcast.6, s32[3,4096]{1,0:T(4,128)} %bitcast.7), custom_call_target="tpu_custom_call" | custom-call | tf_op jit(solution)/shard_map/pallas_call | solution.py:587
  51.8 0.7 %shard_map.68 = (bf16[16,128]{1,0:T(8,128)(2,1)}, bf16[16,4096]{1,0:T(8,128)(2,1)}, f32[8,1,512]{2,1,0:T(1,128)}) custom-call(bf16[16,128]{1,0:T(8,128)(2,1)S(1)} %get-tuple-element.9.refs_0_, bf16[16,4096]{1,0:T(8,128)(2,1)S(1)} %get-tuple-element.10.refs_1_, f32[8,1,512]{2,1,0:T(1,128)S(1)} %get-tuple-element.11.refs_2_), custom_call_target="tpu_custom_call" | custom-call | tf_op jit(solution)/shard_map/pallas_call | solution.py:599

commit v11 on v10

--- a/solution.py
+++ b/solution.py
@@ -384,10 +384,10 @@
     phase("items2_10")
     items(1, core)
     core_send_own(1)
-    items(1, own)
     phase("x2")
     for s in pieces:
         x_send(1, s)
+    items(1, own)
     phase("fwd1_0")
     forward(1, 0)
     acc = user_part(1, own)

time: 52.6 us -> 52.4 us (level)
  no operation moved by 1% of the time
where the time goes in v11:
time: 52.4 us; the launch traced here: 52.2 us
  Pallas kernels  51.6 us (98%)
  between operations  0.64 us (1%)
    pallas_call x1, Pallas kernels, local_fn(): pl.pallas_call(kernel, out_shape=[jax.ShapeDtypeStruct((cols, own_users),...  50.9 us

profile of v11, /device:TPU:0, one launch (start us, length us, event | category | flops | bytes accessed | tf_op | source)
XLA Modules:
  0.0 52.2 jit_solution(10747274703787191035)
XLA Ops:
  0.6 50.9 %shard_map.67 = (bf16[16,128]{1,0:T(8,128)(2,1)S(1)}, bf16[16,4096]{1,0:T(8,128)(2,1)S(1)}, f32[8,1,512]{2,1,0:T(1,128)S(1)}) custom-call(s32[256,16384]{1,0:T(8,128)} %mask_hbm.1, bf16[16,128]{1,0:T(8,128)(2,1)} %bitcast.8, bf16[16,4096]{1,0:T(8,128)(2,1)} %bitcast.6, s32[3,4096]{1,0:T(4,128)} %bitcast.7), custom_call_target="tpu_custom_call" | custom-call | tf_op jit(solution)/shard_map/pallas_call | solution.py:587
  51.6 0.7 %shard_map.68 = (bf16[16,128]{1,0:T(8,128)(2,1)}, bf16[16,4096]{1,0:T(8,128)(2,1)}, f32[8,1,512]{2,1,0:T(1,128)}) custom-call(bf16[16,128]{1,0:T(8,128)(2,1)S(1)} %get-tuple-element.9.refs_0_, bf16[16,4096]{1,0:T(8,128)(2,1)S(1)} %get-tuple-element.10.refs_1_, f32[8,1,512]{2,1,0:T(1,128)S(1)} %get-tuple-element.11.refs_2_), custom_call_target="tpu_custom_call" | custom-call | tf_op jit(solution)/shard_map/pallas_call | solution.py:599
